TPU v7x, 16 devices: a 4x2x1 block of a 4x4x8 slice. The times are simulated.
16 devices in a mesh: dp: 2 (over y, z), tp: 8 (over x, core).
Axes of the slice: x: 4, y: 2, z: 1, core: 2. Of those that a mesh axis runs over, the one named last changes fastest.
The devices are a block of a 4x4x8 slice.
Arguments:
- hidden: bfloat16 [512, 5, 12288], P('dp'), parts along dimension 0
- w_head: bfloat16 [12288, 32768], P(None, 'tp')
- q_draft: float32 [512, 4, 32768], P(('dp', 'tp')), parts along dimension 0
- x_draft: int32 [512, 4], P('dp'), parts along dimension 0
Outputs:
- output 1: float32 [512, 4], P(('dp', 'tp')), parts along dimension 0
- output 2: float32 [512], P(('dp', 'tp')), parts along dimension 0
- output 3: float32 [512, 4, 32768], P(('dp', 'tp')), parts along dimension 0
- output 4: float32 [512, 32768], P(('dp', 'tp')), parts along dimension 0
There are 2 independent parts. A program takes and returns all parts, laid end to end along the dimension named above; an argument that names none is the same for every part.
All inputs are finite; a program needn't handle non-finite values.
Results may differ from a plain program's by a relative error of at most 0.001.
Values are sent between devices in bfloat16 or wider.
A program may use at most 768 MiB of HBM per device.

v0:
```python
import jax
import jax.numpy as jnp
from jax import lax
from jax.sharding import PartitionSpec as P

INV_TEMP = 1.25


def verify_rows(logits, q_rows, x_rows):
    draft_len = q_rows.shape[1]
    row_peak = jnp.max(logits, axis=-1, keepdims=True)
    exp_vals = jnp.exp(logits - row_peak)
    target_p = exp_vals / jnp.sum(exp_vals, axis=-1, keepdims=True)
    draft_p = target_p[:, :draft_len]
    p_pick = jnp.take_along_axis(draft_p, x_rows[:, :, None], axis=2)[:, :, 0]
    q_pick = jnp.take_along_axis(q_rows, x_rows[:, :, None], axis=2)[:, :, 0]
    accept = jnp.minimum(1.0, p_pick / q_pick)
    expected = jnp.sum(jnp.cumprod(accept, axis=1), axis=1)
    excess = jnp.maximum(draft_p - q_rows, 0.0)
    residual = excess / jnp.sum(excess, axis=-1, keepdims=True)
    return accept, expected, residual, target_p[:, draft_len]


def solution(mesh):
    def local_step(hidden, w_shard, q_rows, x_group):
        seq_dev = q_rows.shape[0]
        logits = jnp.einsum("bjd,dv->bjv", hidden, w_shard, preferred_element_type=jnp.float32) * INV_TEMP
        seq_logits = lax.all_to_all(logits, "tp", 0, 2, tiled=True)
        tp_rank = lax.axis_index("tp")
        x_rows = lax.dynamic_slice_in_dim(x_group, tp_rank * seq_dev, seq_dev, axis=0)
        return verify_rows(seq_logits, q_rows, x_rows)

    return jax.shard_map(local_step, mesh=mesh,
                         in_specs=(P("dp", None, None), P(None, "tp"), P(("dp", "tp"), None, None), P("dp", None)),
                         out_specs=(P(("dp", "tp"), None), P(("dp", "tp")), P(("dp", "tp"), None, None), P(("dp", "tp"), None)),
                         check_vma=False)
```

profile of v0, /device:TPU:113, one launch (start us, length us, event | category | flops | bytes accessed | tf_op | source)
XLA Modules:
  0.0 674.1 jit_solution(3179063415179717599)
XLA Ops:
  0.6 144.0 %broadcast_multiply_fusion = f32[256,5,4096]{2,0,1:T(8,128)} fusion(bf16[256,5,12288]{2,0,1:T(8,128)(2,1)} %param.6, bf16[12288,4096]{1,0:T(8,128)(2,1)} %param.7), kind=kOutput, calls=%fused_computation.9 | convolution fusion | flops 128854261760 | bytes 153092096 | tf_op jit(solution)/shard_map/bjd,dv->bjv/dot_general | solution.py:27
  144.7 26.1 %copy.22 = f32[256,5,4096]{2,1,0:T(8,128)} copy(f32[256,5,4096]{2,0,1:T(8,128)} %broadcast_multiply_fusion) | data formatting | bytes 41943040 | tf_op jit(solution)/shard_map/mul | solution.py:27
  170.8 0.0 copy-start.1
  170.8 8.0 %all-to-all-start = ((f32[256,5,4096]{2,1,0:T(8,128)}), f32[256,5,4096]{2,1,0:T(8,128)}, u32[]{:S(2)}, u32[]{:S(2)}) async-start(f32[256,5,4096]{2,1,0:T(8,128)} %copy.22), calls=%async_computation | async-start | bytes 67108864 | tf_op jit(solution)/shard_map/all_to_all | solution.py:28
  178.8 0.0 copy-done.1
  178.8 0.1 fusion.11
  178.9 0.1 copy.24
  179.0 0.1 reshape.51
  179.1 2.3 gather_fusion.1
  181.4 0.1 reshape.60
  181.5 0.1 copy.27
  181.5 360.6 %all-to-all-done = f32[256,5,4096]{2,1,0:T(8,128)} async-done(((f32[256,5,4096]{2,1,0:T(8,128)}), f32[256,5,4096]{2,1,0:T(8,128)}, u32[]{:S(2)}, u32[]{:S(2)}) %all-to-all-start) | async-done | bytes 20971552 | tf_op jit(solution)/shard_map/all_to_all | solution.py:28
  542.1 27.3 %fusion.12 = (f32[32,5]{0,1:T(8,128)S(1)}, f32[32,5,8,4096]{3,2,0,1:T(8,128)}) fusion(f32[8,32,5,4096]{3,2,1,0:T(8,128)} %bitcast.2), kind=kLoop, calls=%fused_computation.26 | loop fusion | flops 5242720 | bytes 41943680 | tf_op jit(solution)/shard_map/reduce_max | solution.py:11
  569.4 22.6 %all_to_all.16 = f32[32,5,32768]{2,0,1:T(8,128)} reshape(f32[32,5,8,4096]{3,2,0,1:T(8,128)} %get-tuple-element.18) | data formatting | bytes 41943040 | tf_op jit(solution)/shard_map/all_to_all | solution.py:28
  592.0 9.2 %exponential_reduce_fusion = f32[32,5]{0,1:T(8,128)S(1)} fusion(f32[32,5,8,4096]{3,2,0,1:T(8,128)} %get-tuple-element.18, f32[32,5]{0,1:T(8,128)S(1)} %get-tuple-element.17), kind=kLoop, calls=%fused_computation.5 | loop fusion | flops 10485600 | bytes 20972800 | tf_op jit(solution)/shard_map/reduce_sum | solution.py:13
  601.1 8.8 %exponential_divide_fusion = f32[32,5,32768]{2,0,1:T(8,128)S(1)} fusion(f32[32,5,32768]{2,0,1:T(8,128)} %all_to_all.16, f32[32,5]{0,1:T(8,128)S(1)} %exponential_reduce_fusion, f32[32,5]{0,1:T(8,128)S(1)} %get-tuple-element.17), kind=kLoop, calls=%fused_computation.6 | loop fusion | flops 10485760 | bytes 41944320 | tf_op jit(solution)/shard_map/div | solution.py:13
  610.0 16.1 %fusion.5 = f32[32,4]{0,1:T(4,128)S(1)} fusion(f32[32,4,32768]{2,1,0:T(4,128)} %param.8, f32[32,5,32768]{2,0,1:T(8,128)S(1)} %exponential_divide_fusion), kind=kLoop, calls=%fused_computation.11 | loop fusion | flops 12582784 | bytes 33554944 | tf_op jit(solution)/shard_map/reduce_sum | solution.py:20
  626.1 2.3 slice_bitcast_fusion
  628.4 21.8 %broadcast_divide_fusion = (f32[32,4,32768]{2,0,1:T(8,128)}, f32[32,4,32768]{2,0,1:T(8,128)}) fusion(f32[32,4]{0,1:T(4,128)S(1)} %fusion.5, f32[32,4,32768]{2,1,0:T(4,128)} %param.8, f32[32,5,32768]{2,0,1:T(8,128)S(1)} %exponential_divide_fusion), kind=kLoop, calls=%fused_computation.10 | loop fusion | flops 12582912 | bytes 67109376 | tf_op jit(solution)/shard_map/div | solution.py:20
  650.1 2.2 gather_fusion
  652.4 0.1 reshape.54
  652.5 0.1 copy.25
  652.6 20.9 %copy.29 = f32[32,4,32768]{2,1,0:T(4,128)} copy(f32[32,4,32768]{2,0,1:T(8,128)} %get-tuple-element.19) | data formatting | bytes 33554432
  673.5 0.1 minimum_bitcast_fusion
  673.6 0.0 copy-start
  673.6 0.5 reduce_sum.28
  674.1 0.0 copy-done
  (5 shorter events, 0.1 us)
Async XLA Ops:
  170.8 8.0 %copy-start.1 = (s32[256,4]{0,1:T(4,128)S(1)}, s32[256,4]{0,1:T(4,128)}, u32[]{:S(2)}) copy-start(s32[256,4]{0,1:T(4,128)} %param.9) | copy-start | bytes 12292
  170.8 371.3 %all-to-all-start = ((f32[256,5,4096]{2,1,0:T(8,128)}), f32[256,5,4096]{2,1,0:T(8,128)}, u32[]{:S(2)}, u32[]{:S(2)}) async-start(f32[256,5,4096]{2,1,0:T(8,128)} %copy.22), calls=%async_computation | async-start | bytes 67108864 | tf_op jit(solution)/shard_map/all_to_all | solution.py:28
  673.6 0.6 copy-start
where the time goes:
time: 676 us; the launch traced here: 674 us
  waiting for transfers between devices  361 us (53%)
  matrix products  144 us (21%)
  other arithmetic  83.9 us (12%)
  local copies, waits for them, and re-layouts  77 us (11%)
  starting transfers between devices  7.98 us (1%)
    all_to_all x1, waiting for transfers between devices, local_step(): seq_logits = lax.all_to_all(logits, 'tp', 0, 2, tiled=True)  361 us
    dot_general x1, matrix products, local_step(): jnp.einsum('bjd,dv->bjv', hidden, w_shard, preferred_element_type=jnp.flo...  144 us
    reduce_max x1, other arithmetic, verify_rows(): row_peak = jnp.max(logits, axis=-1, keepdims=True)  27.3 us
    mul x1, local copies, waits for them, and re-layouts, local_step(): jnp.einsum('bjd,dv->bjv', hidden, w_shard, preferred_element_type=jnp.flo...  26.1 us
    all_to_all x1, local copies, waits for them, and re-layouts, local_step(): seq_logits = lax.all_to_all(logits, 'tp', 0, 2, tiled=True)  22.6 us
    div x1, other arithmetic, verify_rows(): residual = excess / jnp.sum(excess, axis=-1, keepdims=True)  21.8 us
    unnamed x5, local copies, waits for them, and re-layouts  20.9 us
    reduce_sum x1, other arithmetic, verify_rows(): residual = excess / jnp.sum(excess, axis=-1, keepdims=True)  16.1 us
  transfers between devices with their start and end apart: 1, of which 1 were waited for; matrix products, arithmetic and copies ran while one was open for 0% of the time, Pallas kernels for 0%

commit v1 on v0

v1 whole, which is shorter than its diff:
```python
import functools

import jax
import jax.numpy as jnp
from jax import lax
from jax.experimental import pallas as pl
from jax.experimental.pallas import tpu as pltpu
from jax.sharding import PartitionSpec as P

INV_TEMP = 1.25
LANES = 128
TILE = 256
DEPTH = 2048
SLOTS = 4
CORES = 2


def exchange_kernel(draft, n_dev, h_ref, w_ref, zd_ref, zb_ref, st_ref, hbuf, wbuf, acc, stgd, stgb, mrun, srun, stst,
                    hsem, wsem, ssd, ssb, sss, lsd, lsb, lss, rsd, rsb, rss):
    npos = draft + 1
    chips = n_dev // CORES
    seq_chip = h_ref.shape[1] // chips
    seq_dev = seq_chip // CORES
    depth_steps = h_ref.shape[2] // DEPTH
    tiles = w_ref.shape[1] // TILE
    lane_blocks = TILE // LANES
    rows_tile = lane_blocks * draft
    me = lax.axis_index("tp")
    chip, core = me // CORES, lax.rem(me, CORES)
    sib = 1 - core

    order = (1, chips - 1, *range(2, chips - 1), 0)

    def chip_at(ci):
        step = order[ci] if isinstance(ci, int) else ci
        return lax.rem(chip + step, chips)

    def h_copy(ci, k):
        c = chip_at(ci)
        view = (slice(None), pl.ds(pl.multiple_of(c * seq_chip, seq_chip), seq_chip), pl.ds(pl.multiple_of(k * DEPTH, DEPTH), DEPTH))
        return pltpu.make_async_copy(h_ref.at[view], hbuf.at[view], hsem.at[ci, k])

    def w_copy(j, k):
        slot = lax.rem(j, 2)
        rows = pl.ds(pl.multiple_of(k * DEPTH, DEPTH), DEPTH)
        return pltpu.make_async_copy(w_ref.at[rows, pl.ds(pl.multiple_of(j * TILE, TILE), TILE)], wbuf.at[slot, rows], wsem.at[slot, k])

    def part(co):
        return tuple(pl.ds(pl.multiple_of(co * n, n), n) for n in (seq_dev * rows_tile, seq_dev))

    def pieces(j, ci):
        slot = lax.rem(j, SLOTS)
        block = me * tiles + j
        cols = pl.ds(pl.multiple_of(me * tiles * TILE + j * TILE, TILE), TILE)
        out = []
        if order[ci] == 0:
            drows, brows = part(core)
            out.append(pltpu.make_async_copy(stgd.at[slot, ci, drows], zd_ref.at[block], lsd.at[slot]))
            out.append(pltpu.make_async_copy(stgb.at[slot, ci, brows], zb_ref.at[:, cols], lsb.at[slot]))
            cores = (sib,)
        else:
            cores = tuple(range(CORES))
        for n, co in enumerate(cores):
            drows, brows = part(co)
            to = {"tp": chip_at(ci) * CORES + co}
            out.append(pltpu.make_async_remote_copy(stgd.at[slot, ci, drows], zd_ref.at[block], ssd.at[slot, ci, n], rsd.at[me], device_id=to))
            out.append(pltpu.make_async_remote_copy(stgb.at[slot, ci, brows], zb_ref.at[:, cols], ssb.at[slot, ci, n], rsb.at[me], device_id=to))
        return out

    def stat_pieces(ci):
        if order[ci] == 0:
            out = [pltpu.make_async_copy(stst.at[ci, core], st_ref.at[me], lss)]
            cores = (sib,)
        else:
            out = []
            cores = tuple(range(CORES))
        for n, co in enumerate(cores):
            to = {"tp": chip_at(ci) * CORES + co}
            out.append(pltpu.make_async_remote_copy(stst.at[ci, co], st_ref.at[me], sss.at[ci, n], rss.at[me], device_id=to))
        return out

    def wait_sent(copies):
        for copy in copies:
            copy.wait_send() if copy.is_remote else copy.wait()

    for k in range(depth_steps):
        h_copy(0, k).start()
        w_copy(0, k).start()

    barrier = pltpu.get_barrier_semaphore()
    for o in range(1, n_dev):
        pl.semaphore_signal(barrier, 1, device_id={"tp": lax.rem(me + o, n_dev)})
    pl.semaphore_wait(barrier, n_dev - 1)

    mrun[...] = jnp.full(mrun.shape, -jnp.inf, jnp.float32)
    srun[...] = jnp.zeros(srun.shape, jnp.float32)

    @pl.loop(0, tiles)
    def _(j):
        wslot = lax.rem(j, 2)
        slot = lax.rem(j, SLOTS)
        for ci in range(chips):
            start = pl.multiple_of(chip_at(ci) * seq_chip, seq_chip)

            @pl.loop(0, depth_steps)
            def _(k):
                @pl.when(j == 0)
                def _():
                    h_copy(ci, k).wait()
                    if ci + 1 < chips:
                        h_copy(ci + 1, k).start()

                if ci == 0:
                    w_copy(j, k).wait()
                if ci == chips // 2:
                    @pl.when(j + 1 < tiles)
                    def _():
                        w_copy(j + 1, k).start()

                cols = pl.ds(pl.multiple_of(k * DEPTH, DEPTH), DEPTH)
                lhs = hbuf[:, pl.ds(start, seq_chip), cols].reshape(npos * seq_chip, DEPTH)
                prod = jnp.dot(lhs, wbuf[wslot, cols, :], preferred_element_type=jnp.float32)

                @pl.when(k == 0)
                def _():
                    acc[...] = prod

                @pl.when(k > 0)
                def _():
                    acc[...] += prod

            @pl.when(j >= SLOTS)
            def _():
                wait_sent(pieces(j - SLOTS, ci))

            for i in range(npos):
                zs = [acc[i * seq_chip:(i + 1) * seq_chip, cc * LANES:(cc + 1) * LANES] * INV_TEMP for cc in range(lane_blocks)]
                m_old = mrun[ci, i]
                m_new = functools.reduce(jnp.maximum, zs, m_old)
                total = srun[ci, i] * jnp.exp(m_old - m_new)
                for cc, z in enumerate(zs):
                    total += jnp.exp(z - m_new)
                    if i < draft:
                        stgd[slot, ci, pl.ds(cc * draft + i, seq_chip, stride=rows_tile), :] = z
                    else:
                        stgb[slot, ci, :, cc * LANES:(cc + 1) * LANES] = z
                mrun[ci, i] = m_new
                srun[ci, i] = total
            for copy in pieces(j, ci):
                copy.start()

    lane = lax.broadcasted_iota(jnp.int32, (seq_chip, LANES), 1)
    for ci in range(chips):
        packed = jnp.zeros((seq_chip, LANES), jnp.float32)
        for i in range(npos):
            m_lane = mrun[ci, i]
            m = jnp.max(m_lane, axis=1, keepdims=True)
            s = jnp.sum(srun[ci, i] * jnp.exp(m_lane - m), axis=1, keepdims=True)
            packed = jnp.where(lane == i, m, packed)
            packed = jnp.where(lane == 8 + i, s, packed)
        flat = jnp.concatenate([packed, jnp.zeros((LANES - seq_chip, LANES), jnp.float32)], axis=0).T[:16]
        for co in range(CORES):
            stst[ci, co] = flat if co == 0 else pltpu.roll(flat, LANES - co * seq_dev, 1)
        for copy in stat_pieces(ci):
            copy.start()

    for j in range(max(0, tiles - SLOTS), tiles):
        for ci in range(chips):
            wait_sent(pieces(j, ci))
    for ci in range(chips):
        wait_sent(stat_pieces(ci))
    for o in range(1, n_dev):
        src = lax.rem(me + o, n_dev)
        zrows = zd_ref.at[pl.ds(src * tiles, tiles)]
        zcols = zb_ref.at[:, pl.ds(pl.multiple_of(src * tiles * TILE, TILE), tiles * TILE)]
        pltpu.make_async_copy(zrows, zrows, rsd.at[src]).wait()
        pltpu.make_async_copy(zcols, zcols, rsb.at[src]).wait()
        pltpu.make_async_copy(st_ref.at[src], st_ref.at[src], rss.at[src]).wait()


def verify_kernel(draft, x_ref, st_ref, zd_ref, zb_ref, q_ref, acc_ref, exp_ref, res_ref, bon_ref, mrow, irow, mcol, icol):
    step = pl.program_id(0)
    per_step = q_ref.shape[0]
    seq_dev = zb_ref.shape[0]
    first = lax.axis_index("tp") * seq_dev + step * per_step
    lane8 = lax.broadcasted_iota(jnp.int32, (8, LANES), 1)

    @pl.when(step == 0)
    def _():
        m_all = st_ref[:, 0:8, :]
        m = jnp.max(m_all, axis=0)
        s = jnp.sum(st_ref[:, 8:16, :] * jnp.exp(m_all - m[None]), axis=0)
        inv = 1.0 / s
        mrow[...] = jnp.concatenate([m[:draft], m[:draft]], axis=0)
        irow[...] = jnp.concatenate([inv[:draft], inv[:draft]], axis=0)
        pad = jnp.zeros((LANES - 8, LANES), jnp.float32)
        mcol[...] = jnp.broadcast_to(jnp.concatenate([m, pad], axis=0).T[:seq_dev, draft:draft + 1], mcol.shape)
        icol[...] = jnp.broadcast_to(jnp.concatenate([inv, pad], axis=0).T[:seq_dev, draft:draft + 1], icol.shape)
        acc_ref[...] = jnp.zeros(acc_ref.shape, jnp.float32)

    tiles = zd_ref.shape[0]
    group = 8
    seqs = range(per_step)

    def column(ref, bb):
        hit = lane8 == step * per_step + bb
        return jnp.broadcast_to(jnp.sum(jnp.where(hit, ref[...], 0.0), axis=1, keepdims=True), (8, LANES))

    m8 = [column(mrow, bb) for bb in seqs]
    i8 = [column(irow, bb) for bb in seqs]

    def sweep(n, totals):
        out = []
        for bb in seqs:
            total = totals[bb]
            for g in range(group):
                z = zd_ref[n * group + g, bb * 8:(bb + 1) * 8, :]
                at = pl.ds(pl.multiple_of((n * group + g) * 8, 8), 8)
                excess = jnp.maximum(jnp.exp(z - m8[bb]) * i8[bb] - q_ref[bb, at, :], 0.0)
                res_ref[bb, at, :] = excess
                total += excess
            out.append(total)
        return tuple(out)

    totals = lax.fori_loop(0, tiles // group, sweep, tuple(jnp.zeros((8, LANES), jnp.float32) for _ in seqs))
    scales = []
    for total in totals:
        total += pltpu.roll(total, draft, 0)
        scales.append(jnp.broadcast_to(1.0 / jnp.sum(total, axis=1, keepdims=True), (8, LANES)))

    def scale(n, carry):
        for bb in seqs:
            for g in range(group):
                at = pl.ds(pl.multiple_of((n * group + g) * 8, 8), 8)
                res_ref[bb, at, :] = res_ref[bb, at, :] * scales[bb]
        return carry

    lax.fori_loop(0, tiles // group, scale, 0)

    lane1 = lax.broadcasted_iota(jnp.int32, (1, LANES), 1)
    lane_b = lax.broadcasted_iota(jnp.int32, acc_ref.shape, 1)
    picked = acc_ref[...]
    for bb in seqs:
        zs, qs = [], []
        for i in range(draft):
            x = x_ref[i, first + bb]
            pair, half = lax.shift_right_logical(x, 8), lax.shift_right_logical(x, 7) & 1
            row = half * draft + i
            hit = lane1 == (x & (LANES - 1))
            zs.append(jnp.where(hit, zd_ref[pair, pl.ds(bb * 8 + row, 1), :], 0.0))
            qs.append(jnp.where(hit, q_ref[bb, pl.ds(pair * 8 + row, 1), :], 0.0))
        z_pick = jnp.sum(jnp.concatenate(zs, axis=0), axis=1, keepdims=True)
        q_pick = jnp.sum(jnp.concatenate(qs, axis=0), axis=1, keepdims=True)
        ratio = jnp.minimum(1.0, jnp.exp(z_pick - m8[bb][:draft, :1]) * i8[bb][:draft, :1] / q_pick)
        picked = jnp.where(lane_b == step * per_step + bb, ratio, picked)
    acc_ref[...] = picked

    for n in range(zb_ref.shape[1] // LANES):
        at = slice(n * LANES, (n + 1) * LANES)
        bon_ref[:, at] = jnp.exp(zb_ref[:, at] - mcol[...]) * icol[...]

    @pl.when(step == pl.num_programs(0) - 1)
    def _():
        run = acc_ref[0:1, :]
        total = run
        for i in range(1, draft):
            run = run * acc_ref[i:i + 1, :]
            total += run
        exp_ref[...] = total


def solution(mesh):
    n_dev = mesh.shape["tp"]

    def local_step(hidden, w_shard, q_rows, x_group):
        seqs, npos, depth = hidden.shape
        seq_dev, draft, vocab = q_rows.shape
        shard = w_shard.shape[1]
        blocks = vocab // LANES
        chips = n_dev // CORES
        seq_chip = seqs // chips
        f32 = jnp.float32
        dma = pltpu.SemaphoreType.DMA
        rows_tile = TILE // LANES * draft
        ksteps = depth // DEPTH
        any_spec = pl.BlockSpec(memory_space=pl.ANY)
        zd, zb, st = pl.pallas_call(
            functools.partial(exchange_kernel, draft, n_dev),
            out_shape=[jax.ShapeDtypeStruct((vocab // TILE, seq_dev * rows_tile, LANES), f32),
                       jax.ShapeDtypeStruct((seq_dev, vocab), f32),
                       jax.ShapeDtypeStruct((n_dev, 16, LANES), f32)],
            in_specs=[any_spec] * 2,
            out_specs=[any_spec] * 3,
            scratch_shapes=[
                pltpu.VMEM((npos, seqs, depth), hidden.dtype),
                pltpu.VMEM((2, depth, TILE), w_shard.dtype),
                pltpu.VMEM((npos * seq_chip, TILE), f32),
                pltpu.VMEM((SLOTS, chips, seq_chip * rows_tile, LANES), f32),
                pltpu.VMEM((SLOTS, chips, seq_chip, TILE), f32),
                pltpu.VMEM((chips, npos, seq_chip, LANES), f32),
                pltpu.VMEM((chips, npos, seq_chip, LANES), f32),
                pltpu.VMEM((chips, CORES, 16, LANES), f32),
                dma((chips, ksteps)), dma((2, ksteps)),
                dma((SLOTS, chips, CORES)), dma((SLOTS, chips, CORES)), dma((chips, CORES)),
                dma((SLOTS,)), dma((SLOTS,)), dma,
                dma((n_dev,)), dma((n_dev,)), dma((n_dev,)),
            ],
            compiler_params=pltpu.CompilerParams(collective_id=0, has_side_effects=True, vmem_limit_bytes=62 * 1024 * 1024),
            cost_estimate=pl.CostEstimate(flops=2 * seqs * npos * depth * shard, bytes_accessed=2 * depth * shard, transcendentals=0),
            name="head_exchange",
        )(hidden.transpose(1, 0, 2), w_shard)

        q3 = q_rows.reshape(seq_dev, draft, blocks, LANES).transpose(0, 2, 1, 3).reshape(seq_dev, blocks * draft, LANES)
        per_step = 4
        steps = seq_dev // per_step
        row_spec = pl.BlockSpec((per_step, blocks * draft, LANES), lambda s: (s, 0, 0))
        z_spec = pl.BlockSpec((vocab // TILE, per_step * rows_tile, LANES), lambda s: (0, s, 0))
        col_spec = pl.BlockSpec((seq_dev, vocab // steps), lambda s: (0, s))
        accept, expected, res, bonus = pl.pallas_call(
            functools.partial(verify_kernel, draft),
            grid=(steps,),
            out_shape=[jax.ShapeDtypeStruct((draft, seq_dev), f32), jax.ShapeDtypeStruct((1, seq_dev), f32),
                       jax.ShapeDtypeStruct((seq_dev, blocks * draft, LANES), f32), jax.ShapeDtypeStruct((seq_dev, vocab), f32)],
            in_specs=[pl.BlockSpec(memory_space=pltpu.SMEM), pl.BlockSpec((n_dev, 16, LANES), lambda s: (0, 0, 0)), z_spec, col_spec, row_spec],
            out_specs=[pl.BlockSpec((draft, seq_dev), lambda s: (0, 0)), pl.BlockSpec((1, seq_dev), lambda s: (0, 0)), row_spec, col_spec],
            scratch_shapes=[pltpu.VMEM((8, LANES), f32), pltpu.VMEM((8, LANES), f32), pltpu.VMEM((seq_dev, LANES), f32), pltpu.VMEM((seq_dev, LANES), f32)],
            compiler_params=pltpu.CompilerParams(dimension_semantics=("arbitrary",), vmem_limit_bytes=62 * 1024 * 1024),
            cost_estimate=pl.CostEstimate(flops=seq_dev * npos * vocab * 8, bytes_accessed=14 * seq_dev * vocab * 4, transcendentals=seq_dev * npos * vocab),
            name="verify_rows",
        )(x_group.T, st, zd, zb, q3)
        residual = res.reshape(seq_dev, blocks, draft, LANES).transpose(0, 2, 1, 3).reshape(seq_dev, draft, vocab)
        return accept.T, expected.reshape(seq_dev), residual, bonus

    return jax.shard_map(local_step, mesh=mesh,
                         in_specs=(P("dp", None, None), P(None, "tp"), P(("dp", "tp"), None, None), P("dp", None)),
                         out_specs=(P(("dp", "tp"), None), P(("dp", "tp")), P(("dp", "tp"), None, None), P(("dp", "tp"), None)),
                         check_vma=False)
```

time: 676 us -> 264 us (0.39)
  waiting for transfers between devices: 361 us -> 0 us
  Pallas kernels: 0 us -> 263 us
  matrix products: 144 us -> 0 us
  other arithmetic: 83.9 us -> 0 us
  local copies, waits for them, and re-layouts: 77 us -> 0 us
  starting transfers between devices: 7.98 us -> 0 us
    all_to_all x1 -> x0, waiting for transfers between devices: 361 us -> none  [local_step(): seq_logits = lax.all_to_all(logits, 'tp', 0, 2, tiled=True)]
    pallas_call x0 -> x2, Pallas kernels: none -> 263 us  [the longest x1 240 us: local_step(): pl.pallas_call(functools.partial(exchange_kernel, draft, n_dev), out_shap...]
    dot_general x1 -> x0, matrix products: 144 us -> none  [local_step(): jnp.einsum('bjd,dv->bjv', hidden, w_shard, preferred_element_type=jnp.flo...]
    div x2 -> x0, other arithmetic: 30.6 us -> none  [the longest x1 21.8 us: verify_rows(): residual = excess / jnp.sum(excess, axis=-1, keepdims=True)]
    reduce_max x1 -> x0, other arithmetic: 27.3 us -> none  [verify_rows(): row_peak = jnp.max(logits, axis=-1, keepdims=True)]
    mul x1 -> x0, local copies, waits for them, and re-layouts: 26.1 us -> none  [local_step(): jnp.einsum('bjd,dv->bjv', hidden, w_shard, preferred_element_type=jnp.flo...]
    reduce_sum x3 -> x0, other arithmetic: 25.8 us -> none  [the longest x1 16.1 us: verify_rows(): residual = excess / jnp.sum(excess, axis=-1, keepdims=True)]
    all_to_all x1 -> x0, local copies, waits for them, and re-layouts: 22.6 us -> none  [local_step(): seq_logits = lax.all_to_all(logits, 'tp', 0, 2, tiled=True)]
  transfers between devices with their start and end apart: 1 -> 0, of which waited for: 1 -> 0; matrix products, arithmetic and copies ran while one was open for 0% -> 0% of each run, Pallas kernels for 0% -> 0%
where the time goes in v1:
time: 264 us
  Pallas kernels  263 us (100%)
    pallas_call x1, Pallas kernels, local_step(): pl.pallas_call(functools.partial(exchange_kernel, draft, n_dev), out_shap...  240 us
    pallas_call x1, Pallas kernels, local_step(): pl.pallas_call(functools.partial(verify_kernel, draft), grid=(steps,), ou...  23.1 us

profile of v1, /device:TPU:113, one launch (start us, length us, event | category | flops | bytes accessed | tf_op | source)
XLA Modules:
  0.0 263.7 jit_solution(14213229177596026289)
XLA Ops:
  0.6 240.0 %head_exchange.1 = (f32[128,256,128]{2,1,0:T(8,128)}, f32[32,32768]{1,0:T(8,128)}, f32[8,16,128]{2,1,0:T(8,128)}) custom-call(bf16[5,256,12288]{2,1,0:T(8,128)(2,1)} %bitcast.16, bf16[12288,4096]{1,0:T(8,128)(2,1)} %w_ref.1), custom_call_target="tpu_custom_call" | custom-call | flops 128849018880 | bytes 100663296 | tf_op jit(solution)/shard_map/head_exchange/pallas_call | solution.py:287
  240.7 23.1 %verify_rows.1 = (f32[4,32]{1,0:T(4,128)}, f32[1,32]{1,0:T(1,128)}, f32[32,1024,128]{2,1,0:T(8,128)}, f32[32,32768]{1,0:T(8,128)}) custom-call(s32[4,256]{1,0:T(4,128)} %bitcast.15, f32[8,16,128]{2,1,0:T(8,128)} %get-tuple-element.11.st_ref, f32[128,256,128]{2,1,0:T(8,128)} %get-tuple-element.12.zd_ref, f32[32,32768]{1,0:T(8,128)} %get-tuple-element.13.zb_ref, ...), custom_call_target="tpu_custom_call" | custom-call | flops 41943040 | bytes 58720256 | tf_op jit(solution)/shard_map/verify_rows/pallas_call | solution.py:319

commit v2 on v0

v2 whole, which is shorter than its diff:
```python
import functools

import jax
import jax.numpy as jnp
from jax import lax
from jax.experimental import pallas as pl
from jax.experimental.pallas import tpu as pltpu
from jax.sharding import PartitionSpec as P

INV_TEMP = 1.25
LANES = 128
TILE = 256
DEPTH = 2048
SLOTS = 6
CORES = 2
PHASES = 2
UNITS = 2
VMEM_LIMIT = 40 * 1024 * 1024
PEERS = 4


def row_stats(draft, st, seqs):
    m_all = st[:, 0:8, :]
    m = jnp.max(m_all, axis=0)
    inv = 1.0 / jnp.sum(st[:, 8:16, :] * jnp.exp(m_all - m[None]), axis=0)
    rows = [jnp.concatenate([v[:draft], v[:draft]], axis=0) for v in (m, inv)]
    pad = jnp.zeros((LANES - 8, LANES), jnp.float32)
    cols = [jnp.broadcast_to(jnp.concatenate([v, pad], axis=0).T[:seqs, draft:draft + 1], (seqs, LANES)) for v in (m, inv)]
    return rows + cols


def lane_column(rows, lane):
    hit = lax.broadcasted_iota(jnp.int32, (8, LANES), 1) == lane
    return jnp.broadcast_to(jnp.sum(jnp.where(hit, rows, 0.0), axis=1, keepdims=True), (8, LANES))


def inverse_total(draft, total):
    total += pltpu.roll(total, draft, 0)
    return jnp.broadcast_to(1.0 / jnp.sum(total, axis=1, keepdims=True), (8, LANES))


def accept_ratio(draft, tokens, z_row, q_row, m8, i8):
    lane = lax.broadcasted_iota(jnp.int32, (1, LANES), 1)
    zs, qs = [], []
    for i, x in enumerate(tokens):
        pair, half = lax.shift_right_logical(x, 8), lax.shift_right_logical(x, 7) & 1
        hit = lane == (x & (LANES - 1))
        zs.append(jnp.where(hit, z_row(pair, half * draft + i), 0.0))
        qs.append(jnp.where(hit, q_row(pair, half * draft + i), 0.0))
    z = jnp.sum(jnp.concatenate(zs, axis=0), axis=1, keepdims=True)
    q = jnp.sum(jnp.concatenate(qs, axis=0), axis=1, keepdims=True)
    return jnp.minimum(1.0, jnp.exp(z - m8[:draft, :1]) * i8[:draft, :1] / q)


def exchange_kernel(draft, n_dev, h_ref, w_ref, q_ref, x_ref, za_ref, zb_ref, ba_ref, bb_ref, st_ref, acc_ref,
                    hbuf, wbuf, acc, stgd, stgb, mrun, srun, stst, qeven, qodd, mrow, irow, mcol, icol,
                    hsem, wsem, qsem, ssd, ssb, sss, lsd, lsb, lss, rsd, rsb, rss):
    npos = draft + 1
    chips = n_dev // CORES
    seq_dev = h_ref.shape[1] // n_dev
    seq_part = seq_dev // PHASES
    seq_unit = PEERS * seq_part
    depth = h_ref.shape[2]
    depth_steps = depth // DEPTH
    tiles = w_ref.shape[1] // TILE
    lane_blocks = TILE // LANES
    rows_tile = lane_blocks * draft
    me = lax.axis_index("tp")
    chip, core = me // CORES, lax.rem(me, CORES)

    def is_own(u, n):
        return (1 + u + 2 * (n // CORES)) % chips == 0

    def peer(u, n):
        if is_own(u, n):
            return me if n % CORES else me + 1 - 2 * core
        return lax.rem(chip + 1 + u + 2 * (n // CORES), chips) * CORES + n % CORES

    def h_copies(u, p, k):
        cols = pl.ds(pl.multiple_of(k * DEPTH, DEPTH), DEPTH)
        out = []
        for n in range(PEERS):
            rows = pl.ds(pl.multiple_of(peer(u, n) * seq_dev + p * seq_part, seq_part), seq_part)
            out.append(pltpu.make_async_copy(h_ref.at[:, rows, cols], hbuf.at[u, :, n * seq_part:(n + 1) * seq_part, cols], hsem.at[u, n, k]))
        return out

    def w_copy(t, k):
        slot = lax.rem(t, 2)
        rows = pl.ds(pl.multiple_of(k * DEPTH, DEPTH), DEPTH)
        col = pl.multiple_of(lax.rem(t, tiles) * TILE, TILE)
        return pltpu.make_async_copy(w_ref.at[rows, pl.ds(col, TILE)], wbuf.at[slot, rows], wsem.at[slot, k])

    def pieces(t, u, p):
        slot = lax.rem(t, SLOTS)
        block = me * tiles + lax.rem(t, tiles)
        cols = pl.ds(pl.multiple_of(block * TILE, TILE), TILE)
        out = []
        for n in range(PEERS):
            d_src = stgd.at[slot, u, n * seq_part * rows_tile:(n + 1) * seq_part * rows_tile]
            b_src = stgb.at[slot, u, n * seq_part:(n + 1) * seq_part]
            d_dst, b_dst = (za_ref, zb_ref)[p].at[block], (ba_ref, bb_ref)[p].at[:, cols]
            if is_own(u, n) and n % CORES:
                out.append(pltpu.make_async_copy(d_src, d_dst, lsd.at[slot]))
                out.append(pltpu.make_async_copy(b_src, b_dst, lsb.at[slot]))
            else:
                to = {"tp": peer(u, n)}
                out.append(pltpu.make_async_remote_copy(d_src, d_dst, ssd.at[slot, u, n], rsd.at[p, me], device_id=to))
                out.append(pltpu.make_async_remote_copy(b_src, b_dst, ssb.at[slot, u, n], rsb.at[p, me], device_id=to))
        return out

    def stat_pieces(p, u):
        out = []
        for n in range(PEERS):
            src, dst = stst.at[p, u, n], st_ref.at[p, me]
            if is_own(u, n) and n % CORES:
                out.append(pltpu.make_async_copy(src, dst, lss.at[p]))
            else:
                out.append(pltpu.make_async_remote_copy(src, dst, sss.at[p, u, n], rss.at[p, me], device_id={"tp": peer(u, n)}))
        return out

    def wait_sent(copies):
        for copy in copies:
            copy.wait_send() if copy.is_remote else copy.wait()

    def wait_received(p):
        for o in range(1, n_dev):
            src = lax.rem(me + o, n_dev)
            zrows = (za_ref, zb_ref)[p].at[pl.ds(src * tiles, tiles)]
            zcols = (ba_ref, bb_ref)[p].at[:, pl.ds(pl.multiple_of(src * tiles * TILE, TILE), tiles * TILE)]
            pltpu.make_async_copy(zrows, zrows, rsd.at[p, src]).wait()
            pltpu.make_async_copy(zcols, zcols, rsb.at[p, src]).wait()
            pltpu.make_async_copy(st_ref.at[p, src], st_ref.at[p, src], rss.at[p, src]).wait()

    finish_from = tiles + SLOTS + 1

    def q_copy(n, u):
        return pltpu.make_async_copy(q_ref.at[2 * n + u], (qeven, qodd)[u], qsem.at[u])

    def finish(b, q_buf):
        m8, i8 = lane_column(mrow[...], b), lane_column(irow[...], b)
        rows = pl.multiple_of(b * 8, 8)
        first = me * seq_dev + b
        ratio = accept_ratio(draft, [x_ref[i, first] for i in range(draft)],
                             lambda pair, row: za_ref[pair, pl.ds(rows + row, 1), :],
                             lambda pair, row: q_buf[pair, pl.ds(row, 1), :], m8, i8)
        lane = lax.broadcasted_iota(jnp.int32, acc_ref.shape, 1)
        acc_ref[...] = jnp.where(lane == b, ratio, acc_ref[...])
        group = 16
        blocks = za_ref.shape[0]

        def sweep(n, totals):
            totals = list(totals)
            for g in range(group):
                at = n * group + g
                excess = jnp.maximum(jnp.exp(za_ref[at, pl.ds(rows, 8), :] - m8) * i8 - q_buf[at], 0.0)
                za_ref[at, pl.ds(rows, 8), :] = excess
                totals[g % 4] += excess
            return tuple(totals)

        totals = lax.fori_loop(0, blocks // group, sweep, tuple(jnp.zeros((8, LANES), jnp.float32) for _ in range(4)))
        inv = inverse_total(draft, sum(totals))

        def scale(n, carry):
            for g in range(group):
                at = n * group + g
                za_ref[at, pl.ds(rows, 8), :] = za_ref[at, pl.ds(rows, 8), :] * inv
            return carry

        lax.fori_loop(0, blocks // group, scale, 0)
        width = ba_ref.shape[1] // seq_part
        for n in range(width // LANES):
            at = pl.ds(pl.multiple_of(b * width + n * LANES, LANES), LANES)
            ba_ref[:, at] = jnp.exp(ba_ref[:, at] - mcol[...]) * icol[...]

    for k in range(depth_steps):
        for copy in h_copies(0, 0, k):
            copy.start()
        w_copy(0, k).start()

    barrier = pltpu.get_barrier_semaphore()
    for o in range(1, n_dev):
        pl.semaphore_signal(barrier, 1, device_id={"tp": lax.rem(me + o, n_dev)})
    pl.semaphore_wait(barrier, n_dev - 1)

    @pl.loop(0, PHASES * tiles)
    def _(t):
        wslot, slot, p, j = lax.rem(t, 2), lax.rem(t, SLOTS), t // tiles, lax.rem(t, tiles)
        for u in range(UNITS):
            @pl.when(j == 0)
            def _():
                acc[...] = jnp.zeros(acc.shape, jnp.float32)
                mrun[u] = jnp.full(mrun.shape[1:], -jnp.inf, jnp.float32)
                srun[u] = jnp.zeros(srun.shape[1:], jnp.float32)

                @pl.loop(0, depth_steps)
                def _(k):
                    for copy in h_copies(u, p, k):
                        copy.wait()
                    if u + 1 < UNITS:
                        for copy in h_copies(u + 1, p, k):
                            copy.start()
                    if u == 0:
                        w_copy(t, k).wait()
                    else:
                        w_copy(t + 1, k).start()
                    cols = pl.ds(pl.multiple_of(k * DEPTH, DEPTH), DEPTH)
                    acc[...] += jnp.dot(hbuf[u, :, :, cols].reshape(npos * seq_unit, DEPTH), wbuf[wslot, cols, :], preferred_element_type=jnp.float32)

            @pl.when(j > 0)
            def _():
                if u == 0:
                    for k in range(depth_steps):
                        w_copy(t, k).wait()
                else:
                    @pl.when(t + 1 < PHASES * tiles)
                    def _():
                        for k in range(depth_steps):
                            w_copy(t + 1, k).start()
                acc[...] = jnp.dot(hbuf[u].reshape(npos * seq_unit, depth), wbuf[wslot], preferred_element_type=jnp.float32)

            if u == 0:
                @pl.when((j == tiles - 1) & (p + 1 < PHASES))
                def _():
                    for k in range(depth_steps):
                        for copy in h_copies(0, p + 1, k):
                            copy.start()

            @pl.when(t >= SLOTS)
            def _():
                wait_sent(pieces(t - SLOTS, u, 0))

            for i in range(npos):
                zs = [acc[i * seq_unit:(i + 1) * seq_unit, cc * LANES:(cc + 1) * LANES] * INV_TEMP for cc in range(lane_blocks)]
                m_old = mrun[u, i]
                m_new = functools.reduce(jnp.maximum, zs, m_old)
                total = srun[u, i] * jnp.exp(m_old - m_new)
                for cc, z in enumerate(zs):
                    total += jnp.exp(z - m_new)
                    if i < draft:
                        stgd[slot, u, pl.ds(cc * draft + i, seq_unit, stride=rows_tile), :] = z
                    else:
                        stgb[slot, u, :, cc * LANES:(cc + 1) * LANES] = z
                mrun[u, i] = m_new
                srun[u, i] = total
            for static_p in range(PHASES):
                @pl.when(p == static_p)
                def _():
                    for copy in pieces(t, u, static_p):
                        copy.start()

            @pl.when(j == tiles - 1)
            def _():
                lane = lax.broadcasted_iota(jnp.int32, (seq_unit, LANES), 1)
                packed = jnp.zeros((seq_unit, LANES), jnp.float32)
                for i in range(npos):
                    m_lane = mrun[u, i]
                    m = jnp.max(m_lane, axis=1, keepdims=True)
                    s = jnp.sum(srun[u, i] * jnp.exp(m_lane - m), axis=1, keepdims=True)
                    packed = jnp.where(lane == i, m, packed)
                    packed = jnp.where(lane == 8 + i, s, packed)
                flat = jnp.concatenate([packed, jnp.zeros((LANES - seq_unit, LANES), jnp.float32)], axis=0).T[:16]
                for n in range(PEERS):
                    stst[p, u, n] = flat if n == 0 else pltpu.roll(flat, LANES - n * seq_part, 1)
                for copy in stat_pieces(p, u):
                    copy.start()

            @pl.when(t == finish_from - 1)
            def _():
                q_copy(0, u).start()

            @pl.when((t >= finish_from) & (t < finish_from + seq_part // 2))
            def _():
                if u == 0:
                    @pl.when(t == finish_from)
                    def _():
                        for unit in range(UNITS):
                            wait_sent(stat_pieces(0, unit))
                        wait_received(0)
                        for ref, value in zip((mrow, irow, mcol, icol), row_stats(draft, st_ref[0], seq_part)):
                            ref[...] = value
                        acc_ref[...] = jnp.zeros(acc_ref.shape, jnp.float32)
                q_copy(t - finish_from, u).wait()
                finish(2 * (t - finish_from) + u, (qeven, qodd)[u])

                @pl.when(t + 1 < finish_from + seq_part // 2)
                def _():
                    q_copy(t + 1 - finish_from, u).start()

    for t in range(PHASES * tiles - SLOTS, PHASES * tiles):
        for u in range(UNITS):
            wait_sent(pieces(t, u, 1))
    for u in range(UNITS):
        wait_sent(stat_pieces(1, u))
    wait_received(1)


def finish_kernel(draft, x_ref, st_ref, acca_ref, ra_ref, ba_ref, zb_ref, bb_ref, q_ref, acc_ref, exp_ref, res_ref, bon_ref,
                  rb, bonb, mrow, irow, mcol, icol, qsem, rsem, bsem):
    blocks, rows, _ = zb_ref.shape
    seq_part = rows // 8
    group = 4
    first = lax.axis_index("tp") * seq_part * PHASES + seq_part

    def q_copy(b):
        return pltpu.make_async_copy(q_ref.at[seq_part + b], rb.at[b], qsem.at[b])

    def out_copy(b):
        return pltpu.make_async_copy(rb.at[b], res_ref.at[seq_part + b], rsem.at[seq_part + b])

    def out_copy_a(b):
        return pltpu.make_async_copy(ra_ref.at[:, b * 8:(b + 1) * 8], res_ref.at[b], rsem.at[b])

    width = bb_ref.shape[1] // (seq_part // group)

    def bonus_copy(g):
        cols = pl.ds(pl.multiple_of(g * width, width), width)
        return pltpu.make_async_copy(bonb.at[:, cols], bon_ref.at[seq_part:, cols], bsem.at[g + 1])

    bonus_a = pltpu.make_async_copy(ba_ref, bon_ref.at[:seq_part], bsem.at[0])
    for b in range(seq_part):
        q_copy(b).start()
    bonus_a.start()
    for b in range(seq_part):
        out_copy_a(b).start()

    for ref, value in zip((mrow, irow, mcol, icol), row_stats(draft, st_ref[1], seq_part)):
        ref[...] = value
    lane_b = lax.broadcasted_iota(jnp.int32, acc_ref.shape, 1)
    acc_ref[...] = acca_ref[:, :acc_ref.shape[1]]

    @pl.loop(0, seq_part // group)
    def _(g):
        seqs = [g * group + n for n in range(group)]
        m8 = [lane_column(mrow[...], b) for b in seqs]
        i8 = [lane_column(irow[...], b) for b in seqs]
        at_rows = [pl.ds(pl.multiple_of(b * 8, 8), 8) for b in seqs]
        for b in seqs:
            q_copy(b).wait()
        picked = acc_ref[...]
        for n, b in enumerate(seqs):
            ratio = accept_ratio(draft, [x_ref[i, first + b] for i in range(draft)],
                                 lambda pair, row: zb_ref[pair, pl.ds(b * 8 + row, 1), :],
                                 lambda pair, row: rb[b, pair, pl.ds(row, 1), :], m8[n], i8[n])
            picked = jnp.where(lane_b == seq_part + b, ratio, picked)
        acc_ref[...] = picked

        def sweep(k, totals):
            totals = list(totals)
            for n, b in enumerate(seqs):
                for j in range(8):
                    at = k * 8 + j
                    excess = jnp.maximum(jnp.exp(zb_ref[at, at_rows[n], :] - m8[n]) * i8[n] - rb[b, at], 0.0)
                    rb[b, at] = excess
                    totals[n] += excess
            return tuple(totals)

        totals = lax.fori_loop(0, blocks // 8, sweep, tuple(jnp.zeros((8, LANES), jnp.float32) for _ in seqs))
        inv = [inverse_total(draft, total) for total in totals]

        def scale(k, carry):
            for n, b in enumerate(seqs):
                for j in range(8):
                    rb[b, k * 8 + j] = rb[b, k * 8 + j] * inv[n]
            return carry

        lax.fori_loop(0, blocks // 8, scale, 0)
        for b in seqs:
            out_copy(b).start()

        def bonus(k, carry):
            for j in range(8):
                at = pl.ds(pl.multiple_of(g * width + k * 8 * LANES + j * LANES, LANES), LANES)
                bonb[:, at] = jnp.exp(bb_ref[:, at] - mcol[...]) * icol[...]
            return carry

        lax.fori_loop(0, width // (8 * LANES), bonus, 0)
        bonus_copy(g).start()

    run = acc_ref[0:1, :]
    total = run
    for i in range(1, draft):
        run = run * acc_ref[i:i + 1, :]
        total += run
    exp_ref[...] = total

    bonus_a.wait()
    for b in range(seq_part):
        out_copy_a(b).wait()
        out_copy(b).wait()
    for g in range(seq_part // group):
        bonus_copy(g).wait()


def solution(mesh):
    n_dev = mesh.shape["tp"]

    def local_step(hidden, w_shard, q_rows, x_group):
        seqs, npos, depth = hidden.shape
        seq_dev, draft, vocab = q_rows.shape
        shard = w_shard.shape[1]
        blocks = vocab // LANES
        seq_part = seq_dev // PHASES
        seq_unit = PEERS * seq_part
        f32 = jnp.float32
        dma = pltpu.SemaphoreType.DMA
        rows_tile = TILE // LANES * draft
        ksteps = depth // DEPTH
        half_seqs = seq_part * rows_tile
        any_spec = pl.BlockSpec(memory_space=pl.ANY)
        vmem_spec = pl.BlockSpec(memory_space=pltpu.VMEM)
        smem_spec = pl.BlockSpec(memory_space=pltpu.SMEM)
        tokens = x_group.T
        q4 = q_rows.reshape(seq_dev, draft, blocks, LANES).transpose(0, 2, 1, 3).reshape(seq_dev, vocab // TILE, rows_tile, LANES)
        stat_scratch = [pltpu.VMEM((8, LANES), f32)] * 2 + [pltpu.VMEM((seq_part, LANES), f32)] * 2
        res_a, z_b, bon_a, zbon_b, st, acc_a = pl.pallas_call(
            functools.partial(exchange_kernel, draft, n_dev),
            out_shape=[pltpu.VMEM((vocab // TILE, half_seqs, LANES), f32)] * 2 + [pltpu.VMEM((seq_part, vocab), f32)] * 2
                      + [pltpu.VMEM((PHASES, n_dev, 16, LANES), f32), pltpu.VMEM((draft, LANES), f32)],
            in_specs=[any_spec] * 3 + [smem_spec],
            out_specs=[vmem_spec] * 6,
            scratch_shapes=[
                pltpu.VMEM((UNITS, npos, seq_unit, depth), hidden.dtype),
                pltpu.VMEM((2, depth, TILE), w_shard.dtype),
                pltpu.VMEM((npos * seq_unit, TILE), f32),
                pltpu.VMEM((SLOTS, UNITS, seq_unit * rows_tile, LANES), f32),
                pltpu.VMEM((SLOTS, UNITS, seq_unit, TILE), f32),
                pltpu.VMEM((UNITS, npos, seq_unit, LANES), f32),
                pltpu.VMEM((UNITS, npos, seq_unit, LANES), f32),
                pltpu.VMEM((PHASES, UNITS, PEERS, 16, LANES), f32),
                pltpu.VMEM((vocab // TILE, rows_tile, LANES), f32),
                pltpu.VMEM((vocab // TILE, rows_tile, LANES), f32),
                *stat_scratch,
                dma((UNITS, PEERS, ksteps)), dma((2, ksteps)), dma((2,)),
                dma((SLOTS, UNITS, PEERS)), dma((SLOTS, UNITS, PEERS)), dma((PHASES, UNITS, PEERS)),
                dma((SLOTS,)), dma((SLOTS,)), dma((PHASES,)),
                dma((PHASES, n_dev)), dma((PHASES, n_dev)), dma((PHASES, n_dev)),
            ],
            compiler_params=pltpu.CompilerParams(collective_id=0, has_side_effects=True, vmem_limit_bytes=VMEM_LIMIT),
            cost_estimate=pl.CostEstimate(flops=2 * seqs * npos * depth * shard, bytes_accessed=2 * depth * shard, transcendentals=0),
            name="head_exchange",
        )(hidden.transpose(1, 0, 2), w_shard, q4, tokens)

        st, acc_a, res_a, bon_a, z_b, zbon_b = (pltpu.with_memory_space_constraint(v, pltpu.VMEM) for v in (st, acc_a, res_a, bon_a, z_b, zbon_b))
        accept, expected, res, bonus = pl.pallas_call(
            functools.partial(finish_kernel, draft),
            out_shape=[jax.ShapeDtypeStruct((draft, seq_dev), f32), jax.ShapeDtypeStruct((1, seq_dev), f32),
                       jax.ShapeDtypeStruct((seq_dev, vocab // TILE, rows_tile, LANES), f32), jax.ShapeDtypeStruct((seq_dev, vocab), f32)],
            in_specs=[smem_spec] + [vmem_spec] * 6 + [any_spec],
            out_specs=[vmem_spec] * 2 + [any_spec] * 2,
            scratch_shapes=[
                pltpu.VMEM((seq_part, vocab // TILE, rows_tile, LANES), f32), pltpu.VMEM((seq_part, vocab), f32), *stat_scratch,
                dma((seq_part,)), dma((seq_dev,)), dma((seq_part // 4 + 1,)),
            ],
            compiler_params=pltpu.CompilerParams(vmem_limit_bytes=VMEM_LIMIT),
            cost_estimate=pl.CostEstimate(flops=seq_dev * npos * vocab * 8, bytes_accessed=14 * seq_dev * vocab * 4, transcendentals=seq_dev * npos * vocab),
            name="finish_rows",
        )(tokens, st, acc_a, res_a, bon_a, z_b, zbon_b, q4)
        residual = res.reshape(seq_dev, blocks, draft, LANES).transpose(0, 2, 1, 3).reshape(seq_dev, draft, vocab)
        return accept.T, expected.reshape(seq_dev), residual, bonus

    return jax.shard_map(local_step, mesh=mesh,
                         in_specs=(P("dp", None, None), P(None, "tp"), P(("dp", "tp"), None, None), P("dp", None)),
                         out_specs=(P(("dp", "tp"), None), P(("dp", "tp")), P(("dp", "tp"), None, None), P(("dp", "tp"), None)),
                         check_vma=False)
```

time: 676 us -> 254 us (0.38)
  waiting for transfers between devices: 361 us -> 0 us
  Pallas kernels: 0 us -> 254 us
  matrix products: 144 us -> 0 us
  other arithmetic: 83.9 us -> 0 us
  local copies, waits for them, and re-layouts: 77 us -> 0 us
  starting transfers between devices: 7.98 us -> 0 us
    all_to_all x1 -> x0, waiting for transfers between devices: 361 us -> none  [local_step(): seq_logits = lax.all_to_all(logits, 'tp', 0, 2, tiled=True)]
    pallas_call x0 -> x2, Pallas kernels: none -> 254 us  [the longest x1 240 us: local_step(): pl.pallas_call(functools.partial(exchange_kernel, draft, n_dev), out_shap...]
    dot_general x1 -> x0, matrix products: 144 us -> none  [local_step(): jnp.einsum('bjd,dv->bjv', hidden, w_shard, preferred_element_type=jnp.flo...]
    div x2 -> x0, other arithmetic: 30.6 us -> none  [the longest x1 21.8 us: verify_rows(): residual = excess / jnp.sum(excess, axis=-1, keepdims=True)]
    reduce_max x1 -> x0, other arithmetic: 27.3 us -> none  [verify_rows(): row_peak = jnp.max(logits, axis=-1, keepdims=True)]
    mul x1 -> x0, local copies, waits for them, and re-layouts: 26.1 us -> none  [local_step(): jnp.einsum('bjd,dv->bjv', hidden, w_shard, preferred_element_type=jnp.flo...]
    reduce_sum x3 -> x0, other arithmetic: 25.8 us -> none  [the longest x1 16.1 us: verify_rows(): residual = excess / jnp.sum(excess, axis=-1, keepdims=True)]
    all_to_all x1 -> x0, local copies, waits for them, and re-layouts: 22.6 us -> none  [local_step(): seq_logits = lax.all_to_all(logits, 'tp', 0, 2, tiled=True)]
  transfers between devices with their start and end apart: 1 -> 0, of which waited for: 1 -> 0; matrix products, arithmetic and copies ran while one was open for 0% -> 0% of each run, Pallas kernels for 0% -> 0%
where the time goes in v2:
time: 254 us
  Pallas kernels  254 us (100%)
    pallas_call x1, Pallas kernels, local_step(): pl.pallas_call(functools.partial(exchange_kernel, draft, n_dev), out_shap...  240 us
    pallas_call x1, Pallas kernels, local_step(): pl.pallas_call(functools.partial(finish_kernel, draft), out_shape=[jax.Sh...  13.1 us

profile of v2, /device:TPU:113, one launch (start us, length us, event | category | flops | bytes accessed | tf_op | source)
XLA Modules:
  0.0 254.2 jit_solution(5949483427128779702)
XLA Ops:
  0.6 240.4 %head_exchange.1 = (f32[128,128,128]{2,1,0:T(8,128)S(1)}, f32[128,128,128]{2,1,0:T(8,128)S(1)}, f32[16,32768]{1,0:T(8,128)S(1)}, f32[16,32768]{1,0:T(8,128)S(1)}...) custom-call(bf16[5,256,12288]{2,1,0:T(8,128)(2,1)} %bitcast.18, bf16[12288,4096]{1,0:T(8,128)(2,1)} %w_ref.1, ...), custom_call_target="tpu_custom_call" | custom-call | flops 128849018880 | bytes 100663296 | tf_op jit(solution)/shard_map/head_exchange/pallas_call | solution.py:415
  241.1 13.1 %finish_rows.1 = (f32[4,32]{1,0:T(4,128)}, f32[1,32]{1,0:T(1,128)}, f32[32,128,8,128]{3,2,1,0:T(8,128)}, f32[32,32768]{1,0:T(8,128)}) custom-call(s32[4,256]{1,0:T(4,128)} %bitcast.17, f32[2,8,16,128]{3,2,1,0:T(8,128)S(1)} %get-tuple-element.14.st_ref, f32[4,128]{1,0:T(4,128)S(1)} %get-tuple-element.15.acca_ref, ...), custom_call_target="tpu_custom_call" | custom-call | flops 41943040 | bytes 58720256 | tf_op jit(solution)/shard_map/finish_rows/pallas_call | solution.py:444

commit v3 on v2

--- a/solution.py
+++ b/solution.py
@@ -15,14 +15,13 @@
 CORES = 2
 PHASES = 2
 UNITS = 2
-VMEM_LIMIT = 40 * 1024 * 1024
+VMEM_LIMIT = 35 * 1024 * 1024
 PEERS = 4
 
 
 def row_stats(draft, st, seqs):
-    m_all = st[:, 0:8, :]
-    m = jnp.max(m_all, axis=0)
-    inv = 1.0 / jnp.sum(st[:, 8:16, :] * jnp.exp(m_all - m[None]), axis=0)
+    m = functools.reduce(jnp.maximum, st)
+    inv = 1.0 / sum(pltpu.roll(part, LANES - seqs, 1) * jnp.exp(part - m) for part in st)
     rows = [jnp.concatenate([v[:draft], v[:draft]], axis=0) for v in (m, inv)]
     pad = jnp.zeros((LANES - 8, LANES), jnp.float32)
     cols = [jnp.broadcast_to(jnp.concatenate([v, pad], axis=0).T[:seqs, draft:draft + 1], (seqs, LANES)) for v in (m, inv)]
@@ -52,9 +51,9 @@
     return jnp.minimum(1.0, jnp.exp(z - m8[:draft, :1]) * i8[:draft, :1] / q)
 
 
-def exchange_kernel(draft, n_dev, h_ref, w_ref, q_ref, x_ref, za_ref, zb_ref, ba_ref, bb_ref, st_ref, acc_ref,
-                    hbuf, wbuf, acc, stgd, stgb, mrun, srun, stst, qeven, qodd, mrow, irow, mcol, icol,
-                    hsem, wsem, qsem, ssd, ssb, sss, lsd, lsb, lss, rsd, rsb, rss):
+def exchange_kernel(draft, n_dev, h_ref, w_ref, q_ref, x_ref, za_ref, zb_ref, qb_ref, st_ref, acc_ref,
+                    hbuf, wbuf, acc, stage, mrun, srun, stst, qeven, qodd, mrow, irow, mcol, icol,
+                    hsem, wsem, qsem, qbsem, ssd, sss, lsd, lss, rsd, rss):
     npos = draft + 1
     chips = n_dev // CORES
     seq_dev = h_ref.shape[1] // n_dev
@@ -69,12 +68,12 @@
     chip, core = me // CORES, lax.rem(me, CORES)
 
     def is_own(u, n):
-        return (1 + u + 2 * (n // CORES)) % chips == 0
+        return (2 - u + 2 * (n // CORES)) % chips == 0
 
     def peer(u, n):
         if is_own(u, n):
             return me if n % CORES else me + 1 - 2 * core
-        return lax.rem(chip + 1 + u + 2 * (n // CORES), chips) * CORES + n % CORES
+        return lax.rem(chip + 2 - u + 2 * (n // CORES), chips) * CORES + n % CORES
 
     def h_copies(u, p, k):
         cols = pl.ds(pl.multiple_of(k * DEPTH, DEPTH), DEPTH)
@@ -93,19 +92,13 @@
     def pieces(t, u, p):
         slot = lax.rem(t, SLOTS)
         block = me * tiles + lax.rem(t, tiles)
-        cols = pl.ds(pl.multiple_of(block * TILE, TILE), TILE)
         out = []
         for n in range(PEERS):
-            d_src = stgd.at[slot, u, n * seq_part * rows_tile:(n + 1) * seq_part * rows_tile]
-            b_src = stgb.at[slot, u, n * seq_part:(n + 1) * seq_part]
-            d_dst, b_dst = (za_ref, zb_ref)[p].at[block], (ba_ref, bb_ref)[p].at[:, cols]
+            src, dst = stage.at[slot, u, n], (za_ref, zb_ref)[p].at[block]
             if is_own(u, n) and n % CORES:
-                out.append(pltpu.make_async_copy(d_src, d_dst, lsd.at[slot]))
-                out.append(pltpu.make_async_copy(b_src, b_dst, lsb.at[slot]))
+                out.append(pltpu.make_async_copy(src, dst, lsd.at[slot]))
             else:
-                to = {"tp": peer(u, n)}
-                out.append(pltpu.make_async_remote_copy(d_src, d_dst, ssd.at[slot, u, n], rsd.at[p, me], device_id=to))
-                out.append(pltpu.make_async_remote_copy(b_src, b_dst, ssb.at[slot, u, n], rsb.at[p, me], device_id=to))
+                out.append(pltpu.make_async_remote_copy(src, dst, ssd.at[slot, u, n], rsd.at[p, me], device_id={"tp": peer(u, n)}))
         return out
 
     def stat_pieces(p, u):
@@ -126,15 +119,16 @@
         for o in range(1, n_dev):
             src = lax.rem(me + o, n_dev)
             zrows = (za_ref, zb_ref)[p].at[pl.ds(src * tiles, tiles)]
-            zcols = (ba_ref, bb_ref)[p].at[:, pl.ds(pl.multiple_of(src * tiles * TILE, TILE), tiles * TILE)]
             pltpu.make_async_copy(zrows, zrows, rsd.at[p, src]).wait()
-            pltpu.make_async_copy(zcols, zcols, rsb.at[p, src]).wait()
             pltpu.make_async_copy(st_ref.at[p, src], st_ref.at[p, src], rss.at[p, src]).wait()
 
     finish_from = tiles + SLOTS + 1
 
     def q_copy(n, u):
         return pltpu.make_async_copy(q_ref.at[2 * n + u], (qeven, qodd)[u], qsem.at[u])
+
+    def qb_copy(b):
+        return pltpu.make_async_copy(q_ref.at[seq_part + b], qb_ref.at[b], qbsem.at[b])
 
     def finish(b, q_buf):
         m8, i8 = lane_column(mrow[...], b), lane_column(irow[...], b)
@@ -167,10 +161,12 @@
             return carry
 
         lax.fori_loop(0, blocks // group, scale, 0)
-        width = ba_ref.shape[1] // seq_part
-        for n in range(width // LANES):
-            at = pl.ds(pl.multiple_of(b * width + n * LANES, LANES), LANES)
-            ba_ref[:, at] = jnp.exp(ba_ref[:, at] - mcol[...]) * icol[...]
+        part = blocks // seq_part
+        for n in range(part):
+            for row in range(0, seq_part, 8):
+                for cc in range(lane_blocks):
+                    at = pl.ds(seq_part * rows_tile + row * lane_blocks + cc * 8, 8)
+                    za_ref[b * part + n, at, :] = jnp.exp(za_ref[b * part + n, at, :] - mcol[row:row + 8]) * icol[row:row + 8]
 
     for k in range(depth_steps):
         for copy in h_copies(0, 0, k):
@@ -236,10 +232,14 @@
                 total = srun[u, i] * jnp.exp(m_old - m_new)
                 for cc, z in enumerate(zs):
                     total += jnp.exp(z - m_new)
-                    if i < draft:
-                        stgd[slot, u, pl.ds(cc * draft + i, seq_unit, stride=rows_tile), :] = z
-                    else:
-                        stgb[slot, u, :, cc * LANES:(cc + 1) * LANES] = z
+                    for n in range(PEERS):
+                        z_n = z[n * seq_part:(n + 1) * seq_part]
+                        if i < draft:
+                            stage[slot, u, n, pl.ds(cc * draft + i, seq_part, stride=rows_tile), :] = z_n
+                        else:
+                            for row in range(0, seq_part, 8):
+                                at = seq_part * rows_tile + row * lane_blocks + cc * 8
+                                stage[slot, u, n, at:at + 8, :] = z_n[row:row + 8]
                 mrun[u, i] = m_new
                 srun[u, i] = total
             for static_p in range(PHASES):
@@ -260,9 +260,15 @@
                     packed = jnp.where(lane == 8 + i, s, packed)
                 flat = jnp.concatenate([packed, jnp.zeros((LANES - seq_unit, LANES), jnp.float32)], axis=0).T[:16]
                 for n in range(PEERS):
-                    stst[p, u, n] = flat if n == 0 else pltpu.roll(flat, LANES - n * seq_part, 1)
+                    m_n, s_n = (pltpu.roll(v, (LANES - n * seq_part + shift) % LANES, 1) for v, shift in ((flat[:8], 0), (flat[8:], seq_part)))
+                    stst[p, u, n] = jnp.where(lane[:8] < seq_part, m_n, s_n)
                 for copy in stat_pieces(p, u):
                     copy.start()
+
+            if u == 0:
+                @pl.when((t >= tiles) & (t < tiles + seq_part))
+                def _():
+                    qb_copy(t - tiles).start()
 
             @pl.when(t == finish_from - 1)
             def _():
@@ -276,7 +282,7 @@
                         for unit in range(UNITS):
                             wait_sent(stat_pieces(0, unit))
                         wait_received(0)
-                        for ref, value in zip((mrow, irow, mcol, icol), row_stats(draft, st_ref[0], seq_part)):
+                        for ref, value in zip((mrow, irow, mcol, icol), row_stats(draft, [st_ref[0, n] for n in range(n_dev)], seq_part)):
                             ref[...] = value
                         acc_ref[...] = jnp.zeros(acc_ref.shape, jnp.float32)
                 q_copy(t - finish_from, u).wait()
@@ -291,39 +297,45 @@
             wait_sent(pieces(t, u, 1))
     for u in range(UNITS):
         wait_sent(stat_pieces(1, u))
+    for b in range(seq_part):
+        qb_copy(b).wait()
     wait_received(1)
 
 
-def finish_kernel(draft, x_ref, st_ref, acca_ref, ra_ref, ba_ref, zb_ref, bb_ref, q_ref, acc_ref, exp_ref, res_ref, bon_ref,
-                  rb, bonb, mrow, irow, mcol, icol, qsem, rsem, bsem):
-    blocks, rows, _ = zb_ref.shape
-    seq_part = rows // 8
+def finish_kernel(draft, x_ref, st_ref, acca_ref, ra_ref, zb_ref, q_ref, acc_ref, exp_ref, res_ref, bon_ref,
+                  rb, bonb, mrow, irow, mcol, icol, rsem, bsem):
+    blocks = zb_ref.shape[0]
+    seq_part, _, rows_tile, _ = q_ref.shape
+    lane_blocks = rows_tile // draft
+    strips = seq_part // 8
     group = 4
     first = lax.axis_index("tp") * seq_part * PHASES + seq_part
 
-    def q_copy(b):
-        return pltpu.make_async_copy(q_ref.at[seq_part + b], rb.at[b], qsem.at[b])
-
     def out_copy(b):
         return pltpu.make_async_copy(rb.at[b], res_ref.at[seq_part + b], rsem.at[seq_part + b])
 
     def out_copy_a(b):
         return pltpu.make_async_copy(ra_ref.at[:, b * 8:(b + 1) * 8], res_ref.at[b], rsem.at[b])
 
-    width = bb_ref.shape[1] // (seq_part // group)
+    def strip(n):
+        at = seq_part * rows_tile + n * lane_blocks * 8
+        return slice(at, at + lane_blocks * 8)
+
+    def bonus_copy_a(n):
+        return pltpu.make_async_copy(ra_ref.at[:, strip(n)], bon_ref.at[n], bsem.at[n])
+
+    width = blocks // (seq_part // group)
 
     def bonus_copy(g):
-        cols = pl.ds(pl.multiple_of(g * width, width), width)
-        return pltpu.make_async_copy(bonb.at[:, cols], bon_ref.at[seq_part:, cols], bsem.at[g + 1])
-
-    bonus_a = pltpu.make_async_copy(ba_ref, bon_ref.at[:seq_part], bsem.at[0])
-    for b in range(seq_part):
-        q_copy(b).start()
-    bonus_a.start()
+        at = pl.ds(g * width, width)
+        return pltpu.make_async_copy(bonb.at[:, at], bon_ref.at[strips:, at], bsem.at[strips + g])
+
     for b in range(seq_part):
         out_copy_a(b).start()
-
-    for ref, value in zip((mrow, irow, mcol, icol), row_stats(draft, st_ref[1], seq_part)):
+    for n in range(strips):
+        bonus_copy_a(n).start()
+
+    for ref, value in zip((mrow, irow, mcol, icol), row_stats(draft, [st_ref[1, n] for n in range(st_ref.shape[1])], seq_part)):
         ref[...] = value
     lane_b = lax.broadcasted_iota(jnp.int32, acc_ref.shape, 1)
     acc_ref[...] = acca_ref[:, :acc_ref.shape[1]]
@@ -334,13 +346,11 @@
         m8 = [lane_column(mrow[...], b) for b in seqs]
         i8 = [lane_column(irow[...], b) for b in seqs]
         at_rows = [pl.ds(pl.multiple_of(b * 8, 8), 8) for b in seqs]
-        for b in seqs:
-            q_copy(b).wait()
         picked = acc_ref[...]
         for n, b in enumerate(seqs):
             ratio = accept_ratio(draft, [x_ref[i, first + b] for i in range(draft)],
                                  lambda pair, row: zb_ref[pair, pl.ds(b * 8 + row, 1), :],
-                                 lambda pair, row: rb[b, pair, pl.ds(row, 1), :], m8[n], i8[n])
+                                 lambda pair, row: q_ref[b, pair, pl.ds(row, 1), :], m8[n], i8[n])
             picked = jnp.where(lane_b == seq_part + b, ratio, picked)
         acc_ref[...] = picked
 
@@ -349,7 +359,7 @@
             for n, b in enumerate(seqs):
                 for j in range(8):
                     at = k * 8 + j
-                    excess = jnp.maximum(jnp.exp(zb_ref[at, at_rows[n], :] - m8[n]) * i8[n] - rb[b, at], 0.0)
+                    excess = jnp.maximum(jnp.exp(zb_ref[at, at_rows[n], :] - m8[n]) * i8[n] - q_ref[b, at], 0.0)
                     rb[b, at] = excess
                     totals[n] += excess
             return tuple(totals)
@@ -368,12 +378,15 @@
             out_copy(b).start()
 
         def bonus(k, carry):
-            for j in range(8):
-                at = pl.ds(pl.multiple_of(g * width + k * 8 * LANES + j * LANES, LANES), LANES)
-                bonb[:, at] = jnp.exp(bb_ref[:, at] - mcol[...]) * icol[...]
+            at = g * width + k
+            for n in range(strips):
+                for cc in range(lane_blocks):
+                    row = strip(n).start + cc * 8
+                    seqs8 = slice(n * 8, (n + 1) * 8)
+                    bonb[n, at, cc * 8:(cc + 1) * 8, :] = jnp.exp(zb_ref[at, row:row + 8, :] - mcol[seqs8]) * icol[seqs8]
             return carry
 
-        lax.fori_loop(0, width // (8 * LANES), bonus, 0)
+        lax.fori_loop(0, width, bonus, 0, unroll=4)
         bonus_copy(g).start()
 
     run = acc_ref[0:1, :]
@@ -383,7 +396,8 @@
         total += run
     exp_ref[...] = total
 
-    bonus_a.wait()
+    for n in range(strips):
+        bonus_copy_a(n).wait()
     for b in range(seq_part):
         out_copy_a(b).wait()
         out_copy(b).wait()
@@ -405,58 +419,57 @@
         dma = pltpu.SemaphoreType.DMA
         rows_tile = TILE // LANES * draft
         ksteps = depth // DEPTH
-        half_seqs = seq_part * rows_tile
+        rows_block = seq_part * (rows_tile + TILE // LANES)
         any_spec = pl.BlockSpec(memory_space=pl.ANY)
         vmem_spec = pl.BlockSpec(memory_space=pltpu.VMEM)
         smem_spec = pl.BlockSpec(memory_space=pltpu.SMEM)
         tokens = x_group.T
         q4 = q_rows.reshape(seq_dev, draft, blocks, LANES).transpose(0, 2, 1, 3).reshape(seq_dev, vocab // TILE, rows_tile, LANES)
         stat_scratch = [pltpu.VMEM((8, LANES), f32)] * 2 + [pltpu.VMEM((seq_part, LANES), f32)] * 2
-        res_a, z_b, bon_a, zbon_b, st, acc_a = pl.pallas_call(
+        res_a, z_b, q_b, st, acc_a = pl.pallas_call(
             functools.partial(exchange_kernel, draft, n_dev),
-            out_shape=[pltpu.VMEM((vocab // TILE, half_seqs, LANES), f32)] * 2 + [pltpu.VMEM((seq_part, vocab), f32)] * 2
-                      + [pltpu.VMEM((PHASES, n_dev, 16, LANES), f32), pltpu.VMEM((draft, LANES), f32)],
+            out_shape=[pltpu.VMEM((vocab // TILE, rows_block, LANES), f32)] * 2 + [pltpu.VMEM((seq_part, vocab // TILE, rows_tile, LANES), f32)]
+                      + [pltpu.VMEM((PHASES, n_dev, 8, LANES), f32), pltpu.VMEM((draft, LANES), f32)],
             in_specs=[any_spec] * 3 + [smem_spec],
-            out_specs=[vmem_spec] * 6,
+            out_specs=[vmem_spec] * 5,
             scratch_shapes=[
                 pltpu.VMEM((UNITS, npos, seq_unit, depth), hidden.dtype),
                 pltpu.VMEM((2, depth, TILE), w_shard.dtype),
                 pltpu.VMEM((npos * seq_unit, TILE), f32),
-                pltpu.VMEM((SLOTS, UNITS, seq_unit * rows_tile, LANES), f32),
-                pltpu.VMEM((SLOTS, UNITS, seq_unit, TILE), f32),
+                pltpu.VMEM((SLOTS, UNITS, PEERS, rows_block, LANES), f32),
                 pltpu.VMEM((UNITS, npos, seq_unit, LANES), f32),
                 pltpu.VMEM((UNITS, npos, seq_unit, LANES), f32),
-                pltpu.VMEM((PHASES, UNITS, PEERS, 16, LANES), f32),
+                pltpu.VMEM((PHASES, UNITS, PEERS, 8, LANES), f32),
                 pltpu.VMEM((vocab // TILE, rows_tile, LANES), f32),
                 pltpu.VMEM((vocab // TILE, rows_tile, LANES), f32),
                 *stat_scratch,
-                dma((UNITS, PEERS, ksteps)), dma((2, ksteps)), dma((2,)),
-                dma((SLOTS, UNITS, PEERS)), dma((SLOTS, UNITS, PEERS)), dma((PHASES, UNITS, PEERS)),
-                dma((SLOTS,)), dma((SLOTS,)), dma((PHASES,)),
-                dma((PHASES, n_dev)), dma((PHASES, n_dev)), dma((PHASES, n_dev)),
+                dma((UNITS, PEERS, ksteps)), dma((2, ksteps)), dma((2,)), dma((seq_part,)),
+                dma((SLOTS, UNITS, PEERS)), dma((PHASES, UNITS, PEERS)), dma((SLOTS,)), dma((PHASES,)),
+                dma((PHASES, n_dev)), dma((PHASES, n_dev)),
             ],
             compiler_params=pltpu.CompilerParams(collective_id=0, has_side_effects=True, vmem_limit_bytes=VMEM_LIMIT),
             cost_estimate=pl.CostEstimate(flops=2 * seqs * npos * depth * shard, bytes_accessed=2 * depth * shard, transcendentals=0),
             name="head_exchange",
         )(hidden.transpose(1, 0, 2), w_shard, q4, tokens)
 
-        st, acc_a, res_a, bon_a, z_b, zbon_b = (pltpu.with_memory_space_constraint(v, pltpu.VMEM) for v in (st, acc_a, res_a, bon_a, z_b, zbon_b))
+        st, acc_a, res_a, z_b, q_b = (pltpu.with_memory_space_constraint(v, pltpu.VMEM) for v in (st, acc_a, res_a, z_b, q_b))
         accept, expected, res, bonus = pl.pallas_call(
             functools.partial(finish_kernel, draft),
             out_shape=[jax.ShapeDtypeStruct((draft, seq_dev), f32), jax.ShapeDtypeStruct((1, seq_dev), f32),
-                       jax.ShapeDtypeStruct((seq_dev, vocab // TILE, rows_tile, LANES), f32), jax.ShapeDtypeStruct((seq_dev, vocab), f32)],
-            in_specs=[smem_spec] + [vmem_spec] * 6 + [any_spec],
+                       jax.ShapeDtypeStruct((seq_dev, vocab // TILE, rows_tile, LANES), f32),
+                       jax.ShapeDtypeStruct((seq_dev // 8, vocab // TILE, TILE // LANES * 8, LANES), f32)],
+            in_specs=[smem_spec] + [vmem_spec] * 5,
             out_specs=[vmem_spec] * 2 + [any_spec] * 2,
             scratch_shapes=[
-                pltpu.VMEM((seq_part, vocab // TILE, rows_tile, LANES), f32), pltpu.VMEM((seq_part, vocab), f32), *stat_scratch,
-                dma((seq_part,)), dma((seq_dev,)), dma((seq_part // 4 + 1,)),
+                pltpu.VMEM((seq_part, vocab // TILE, rows_tile, LANES), f32), pltpu.VMEM((seq_part // 8, vocab // TILE, TILE // LANES * 8, LANES), f32), *stat_scratch,
+                dma((seq_dev,)), dma((seq_part // 8 + seq_part // 4,)),
             ],
             compiler_params=pltpu.CompilerParams(vmem_limit_bytes=VMEM_LIMIT),
             cost_estimate=pl.CostEstimate(flops=seq_dev * npos * vocab * 8, bytes_accessed=14 * seq_dev * vocab * 4, transcendentals=seq_dev * npos * vocab),
             name="finish_rows",
-        )(tokens, st, acc_a, res_a, bon_a, z_b, zbon_b, q4)
+        )(tokens, st, acc_a, res_a, z_b, q_b)
         residual = res.reshape(seq_dev, blocks, draft, LANES).transpose(0, 2, 1, 3).reshape(seq_dev, draft, vocab)
-        return accept.T, expected.reshape(seq_dev), residual, bonus
+        return accept.T, expected.reshape(seq_dev), residual, bonus.reshape(seq_dev // 8, vocab // TILE, TILE // LANES, 8, LANES).transpose(0, 3, 1, 2, 4).reshape(seq_dev, vocab)
 
     return jax.shard_map(local_step, mesh=mesh,
                          in_specs=(P("dp", None, None), P(None, "tp"), P(("dp", "tp"), None, None), P("dp", None)),

time: 254 us -> 248 us (0.976)
  Pallas kernels: 254 us -> 248 us
    pallas_call x1, Pallas kernels: 13.1 us -> 8.7 us  [local_step(): pl.pallas_call(functools.partial(finish_kernel, draft), out_shape=[jax.Sh...]
where the time goes in v3:
time: 248 us
  Pallas kernels  248 us (100%)
    pallas_call x1, Pallas kernels, local_step(): pl.pallas_call(functools.partial(exchange_kernel, draft, n_dev), out_shap...  239 us
    pallas_call x1, Pallas kernels, local_step(): pl.pallas_call(functools.partial(finish_kernel, draft), out_shape=[jax.Sh...  8.7 us

profile of v3, /device:TPU:113, one launch (start us, length us, event | category | flops | bytes accessed | tf_op | source)
XLA Modules:
  0.0 248.2 jit_solution(9908682195878712448)
XLA Ops:
  0.6 238.8 %head_exchange.1 = (f32[128,160,128]{2,1,0:T(8,128)S(1)}, f32[128,160,128]{2,1,0:T(8,128)S(1)}, f32[16,128,8,128]{3,2,1,0:T(8,128)S(1)}, f32[2,8,8,128]{3,2,1,0:T(8,128)S(1)}, f32[4,128]{1,0:T(4,128)S(1)}) custom-call(bf16[5,256,12288]{2,1,0:T(8,128)(2,1)} %bitcast.21, bf16[12288,4096]{1,0:T(8,128)(2,1)} %w_ref.1, f32[32,128,8,128]{3,2,1,0:T(8,128)} %bitcast.22, ...), custom_call_target="tpu_custom_call" | custom-call | flops 128849018880 | bytes 100663296 | tf_op jit(solution)/shard_map/head_exchange/pallas_call | solution.py:429
  239.5 8.7 %finish_rows.1 = (f32[4,32]{1,0:T(4,128)}, f32[1,32]{1,0:T(1,128)}, f32[32,128,8,128]{3,2,1,0:T(8,128)}, f32[4,128,16,128]{3,2,1,0:T(8,128)}) custom-call(s32[4,256]{1,0:T(4,128)} %bitcast.20, f32[2,8,8,128]{3,2,1,0:T(8,128)S(1)} %get-tuple-element.13.st_ref, f32[4,128]{1,0:T(4,128)S(1)} %get-tuple-element.14.acca_ref, ...), custom_call_target="tpu_custom_call" | custom-call | flops 41943040 | bytes 58720256 | tf_op jit(solution)/shard_map/finish_rows/pallas_call | solution.py:456

commit v4 on v3

--- a/solution.py
+++ b/solution.py
@@ -10,7 +10,7 @@
 INV_TEMP = 1.25
 LANES = 128
 TILE = 256
-DEPTH = 2048
+DEPTH = 3072
 SLOTS = 6
 CORES = 2
 PHASES = 2
@@ -75,10 +75,10 @@
             return me if n % CORES else me + 1 - 2 * core
         return lax.rem(chip + 2 - u + 2 * (n // CORES), chips) * CORES + n % CORES
 
-    def h_copies(u, p, k):
+    def h_copies(u, p, k, peers):
         cols = pl.ds(pl.multiple_of(k * DEPTH, DEPTH), DEPTH)
         out = []
-        for n in range(PEERS):
+        for n in peers:
             rows = pl.ds(pl.multiple_of(peer(u, n) * seq_dev + p * seq_part, seq_part), seq_part)
             out.append(pltpu.make_async_copy(h_ref.at[:, rows, cols], hbuf.at[u, :, n * seq_part:(n + 1) * seq_part, cols], hsem.at[u, n, k]))
         return out
@@ -89,11 +89,11 @@
         col = pl.multiple_of(lax.rem(t, tiles) * TILE, TILE)
         return pltpu.make_async_copy(w_ref.at[rows, pl.ds(col, TILE)], wbuf.at[slot, rows], wsem.at[slot, k])
 
-    def pieces(t, u, p):
+    def pieces(t, u, p, peers):
         slot = lax.rem(t, SLOTS)
         block = me * tiles + lax.rem(t, tiles)
         out = []
-        for n in range(PEERS):
+        for n in peers:
             src, dst = stage.at[slot, u, n], (za_ref, zb_ref)[p].at[block]
             if is_own(u, n) and n % CORES:
                 out.append(pltpu.make_async_copy(src, dst, lsd.at[slot]))
@@ -168,9 +168,15 @@
                     at = pl.ds(seq_part * rows_tile + row * lane_blocks + cc * 8, 8)
                     za_ref[b * part + n, at, :] = jnp.exp(za_ref[b * part + n, at, :] - mcol[row:row + 8]) * icol[row:row + 8]
 
+    everyone, far, own = tuple(range(PEERS)), tuple(range(CORES)), tuple(range(CORES, PEERS))
+    last = PHASES * tiles - 1
+
+    def start_all(copies):
+        for copy in copies:
+            copy.start()
+
     for k in range(depth_steps):
-        for copy in h_copies(0, 0, k):
-            copy.start()
+        start_all(h_copies(0, 0, k, far))
         w_copy(0, k).start()
 
     barrier = pltpu.get_barrier_semaphore()
@@ -178,75 +184,114 @@
         pl.semaphore_signal(barrier, 1, device_id={"tp": lax.rem(me + o, n_dev)})
     pl.semaphore_wait(barrier, n_dev - 1)
 
+    def multiply_as_it_comes(t, u, peers):
+        p = t // tiles
+        rows = slice(peers[0] * seq_part, (peers[-1] + 1) * seq_part)
+        count = len(peers) * seq_part
+        acc[:, rows, :] = jnp.zeros((npos, count, TILE), jnp.float32)
+        mrun[u] = jnp.full(mrun.shape[1:], -jnp.inf, jnp.float32)
+        srun[u] = jnp.zeros(srun.shape[1:], jnp.float32)
+
+        @pl.loop(0, depth_steps)
+        def _(k):
+            for copy in h_copies(u, p, k, peers):
+                copy.wait()
+            if peers == far:
+                w_copy(t, k).wait()
+                start_all(h_copies(1, p, k, everyone))
+            else:
+                start_all(h_copies(0, p, k, own))
+                w_copy(t + 1, k).start()
+            cols = pl.ds(pl.multiple_of(k * DEPTH, DEPTH), DEPTH)
+            lhs = hbuf[u, :, rows, cols].reshape(npos * count, DEPTH)
+            prod = jnp.dot(lhs, wbuf[lax.rem(t, 2), cols, :], preferred_element_type=jnp.float32)
+            acc[:, rows, :] += prod.reshape(npos, count, TILE)
+
+    def multiply(t, u):
+        if u == 0:
+            for k in range(depth_steps):
+                w_copy(t, k).wait()
+        else:
+            @pl.when(t < last)
+            def _():
+                for k in range(depth_steps):
+                    w_copy(t + 1, k).start()
+        prod = jnp.dot(hbuf[u].reshape(npos * seq_unit, depth), wbuf[lax.rem(t, 2)], preferred_element_type=jnp.float32)
+        acc[...] = prod.reshape(acc.shape)
+
+    def multiply_own(t):
+        rows = slice(CORES * seq_part, seq_unit)
+        count = seq_unit - CORES * seq_part
+        prod = jnp.dot(hbuf[0, :, rows].reshape(npos * count, depth), wbuf[lax.rem(t, 2)], preferred_element_type=jnp.float32)
+        acc[:, rows, :] = prod.reshape(npos, count, TILE)
+
+    def send(t, u, peers):
+        slot, p = lax.rem(t, SLOTS), t // tiles
+
+        @pl.when(t >= SLOTS)
+        def _():
+            wait_sent(pieces(t - SLOTS, u, 0, peers))
+
+        rows = slice(peers[0] * seq_part, (peers[-1] + 1) * seq_part)
+        for i in range(npos):
+            zs = [acc[i, rows, cc * LANES:(cc + 1) * LANES] * INV_TEMP for cc in range(lane_blocks)]
+            m_old = mrun[u, i, rows]
+            m_new = functools.reduce(jnp.maximum, zs, m_old)
+            total = srun[u, i, rows] * jnp.exp(m_old - m_new)
+            for cc, z in enumerate(zs):
+                total += jnp.exp(z - m_new)
+                for at_n, n in enumerate(peers):
+                    z_n = z[at_n * seq_part:(at_n + 1) * seq_part]
+                    if i < draft:
+                        stage[slot, u, n, pl.ds(cc * draft + i, seq_part, stride=rows_tile), :] = z_n
+                    else:
+                        for row in range(0, seq_part, 8):
+                            at = seq_part * rows_tile + row * lane_blocks + cc * 8
+                            stage[slot, u, n, at:at + 8, :] = z_n[row:row + 8]
+            mrun[u, i, rows] = m_new
+            srun[u, i, rows] = total
+        for static_p in range(PHASES):
+            @pl.when(p == static_p)
+            def _():
+                start_all(pieces(t, u, static_p, peers))
+
     @pl.loop(0, PHASES * tiles)
     def _(t):
-        wslot, slot, p, j = lax.rem(t, 2), lax.rem(t, SLOTS), t // tiles, lax.rem(t, tiles)
+        p, j = t // tiles, lax.rem(t, tiles)
         for u in range(UNITS):
+            peers = far if u == 0 else everyone
+
             @pl.when(j == 0)
             def _():
-                acc[...] = jnp.zeros(acc.shape, jnp.float32)
-                mrun[u] = jnp.full(mrun.shape[1:], -jnp.inf, jnp.float32)
-                srun[u] = jnp.zeros(srun.shape[1:], jnp.float32)
-
-                @pl.loop(0, depth_steps)
-                def _(k):
-                    for copy in h_copies(u, p, k):
-                        copy.wait()
-                    if u + 1 < UNITS:
-                        for copy in h_copies(u + 1, p, k):
-                            copy.start()
-                    if u == 0:
-                        w_copy(t, k).wait()
-                    else:
-                        w_copy(t + 1, k).start()
-                    cols = pl.ds(pl.multiple_of(k * DEPTH, DEPTH), DEPTH)
-                    acc[...] += jnp.dot(hbuf[u, :, :, cols].reshape(npos * seq_unit, DEPTH), wbuf[wslot, cols, :], preferred_element_type=jnp.float32)
+                multiply_as_it_comes(t, u, peers)
+
+            if u == 0:
+                @pl.when(j == 1)
+                def _():
+                    for k in range(depth_steps):
+                        for copy in h_copies(0, p, k, own):
+                            copy.wait()
 
             @pl.when(j > 0)
             def _():
-                if u == 0:
-                    for k in range(depth_steps):
-                        w_copy(t, k).wait()
-                else:
-                    @pl.when(t + 1 < PHASES * tiles)
-                    def _():
-                        for k in range(depth_steps):
-                            w_copy(t + 1, k).start()
-                acc[...] = jnp.dot(hbuf[u].reshape(npos * seq_unit, depth), wbuf[wslot], preferred_element_type=jnp.float32)
+                multiply(t, u)
 
             if u == 0:
                 @pl.when((j == tiles - 1) & (p + 1 < PHASES))
                 def _():
                     for k in range(depth_steps):
-                        for copy in h_copies(0, p + 1, k):
-                            copy.start()
-
-            @pl.when(t >= SLOTS)
-            def _():
-                wait_sent(pieces(t - SLOTS, u, 0))
-
-            for i in range(npos):
-                zs = [acc[i * seq_unit:(i + 1) * seq_unit, cc * LANES:(cc + 1) * LANES] * INV_TEMP for cc in range(lane_blocks)]
-                m_old = mrun[u, i]
-                m_new = functools.reduce(jnp.maximum, zs, m_old)
-                total = srun[u, i] * jnp.exp(m_old - m_new)
-                for cc, z in enumerate(zs):
-                    total += jnp.exp(z - m_new)
-                    for n in range(PEERS):
-                        z_n = z[n * seq_part:(n + 1) * seq_part]
-                        if i < draft:
-                            stage[slot, u, n, pl.ds(cc * draft + i, seq_part, stride=rows_tile), :] = z_n
-                        else:
-                            for row in range(0, seq_part, 8):
-                                at = seq_part * rows_tile + row * lane_blocks + cc * 8
-                                stage[slot, u, n, at:at + 8, :] = z_n[row:row + 8]
-                mrun[u, i] = m_new
-                srun[u, i] = total
-            for static_p in range(PHASES):
-                @pl.when(p == static_p)
+                        start_all(h_copies(0, p + 1, k, far))
+
+            send(t, u, peers)
+            if u == 0:
+                @pl.when(j > 0)
                 def _():
-                    for copy in pieces(t, u, static_p):
-                        copy.start()
+                    send(t, 0, own)
+
+                @pl.when(j == 1)
+                def _():
+                    multiply_own(t - 1)
+                    send(t - 1, 0, own)
 
             @pl.when(j == tiles - 1)
             def _():
@@ -294,7 +339,7 @@
 
     for t in range(PHASES * tiles - SLOTS, PHASES * tiles):
         for u in range(UNITS):
-            wait_sent(pieces(t, u, 1))
+            wait_sent(pieces(t, u, 1, everyone))
     for u in range(UNITS):
         wait_sent(stat_pieces(1, u))
     for b in range(seq_part):
@@ -435,7 +480,7 @@
             scratch_shapes=[
                 pltpu.VMEM((UNITS, npos, seq_unit, depth), hidden.dtype),
                 pltpu.VMEM((2, depth, TILE), w_shard.dtype),
-                pltpu.VMEM((npos * seq_unit, TILE), f32),
+                pltpu.VMEM((npos, seq_unit, TILE), f32),
                 pltpu.VMEM((SLOTS, UNITS, PEERS, rows_block, LANES), f32),
                 pltpu.VMEM((UNITS, npos, seq_unit, LANES), f32),
                 pltpu.VMEM((UNITS, npos, seq_unit, LANES), f32),

time: 248 us -> 247 us (level)
  no operation moved by 1% of the time
where the time goes in v4:
time: 247 us
  Pallas kernels  246 us (100%)
    pallas_call x1, Pallas kernels, local_step(): pl.pallas_call(functools.partial(exchange_kernel, draft, n_dev), out_shap...  238 us
    pallas_call x1, Pallas kernels, local_step(): pl.pallas_call(functools.partial(finish_kernel, draft), out_shape=[jax.Sh...  8.7 us

profile of v4, /device:TPU:113, one launch (start us, length us, event | category | flops | bytes accessed | tf_op | source)
XLA Modules:
  0.0 247.1 jit_solution(18100765556292539039)
XLA Ops:
  0.6 237.8 %head_exchange.1 = (f32[128,160,128]{2,1,0:T(8,128)S(1)}, f32[128,160,128]{2,1,0:T(8,128)S(1)}, f32[16,128,8,128]{3,2,1,0:T(8,128)S(1)}, f32[2,8,8,128]{3,2,1,0:T(8,128)S(1)}, f32[4,128]{1,0:T(4,128)S(1)}) custom-call(bf16[5,256,12288]{2,1,0:T(8,128)(2,1)} %bitcast.21, bf16[12288,4096]{1,0:T(8,128)(2,1)} %w_ref.1, f32[32,128,8,128]{3,2,1,0:T(8,128)} %bitcast.22, ...), custom_call_target="tpu_custom_call" | custom-call | flops 128849018880 | bytes 100663296 | tf_op jit(solution)/shard_map/head_exchange/pallas_call | solution.py:474
  238.4 8.7 %finish_rows.1 = (f32[4,32]{1,0:T(4,128)}, f32[1,32]{1,0:T(1,128)}, f32[32,128,8,128]{3,2,1,0:T(8,128)}, f32[4,128,16,128]{3,2,1,0:T(8,128)}) custom-call(s32[4,256]{1,0:T(4,128)} %bitcast.20, f32[2,8,8,128]{3,2,1,0:T(8,128)S(1)} %get-tuple-element.13.st_ref, f32[4,128]{1,0:T(4,128)S(1)} %get-tuple-element.14.acca_ref, ...), custom_call_target="tpu_custom_call" | custom-call | flops 41943040 | bytes 58720256 | tf_op jit(solution)/shard_map/finish_rows/pallas_call | solution.py:501

commit v5 on v4

--- a/solution.py
+++ b/solution.py
@@ -52,8 +52,8 @@
 
 
 def exchange_kernel(draft, n_dev, h_ref, w_ref, q_ref, x_ref, za_ref, zb_ref, qb_ref, st_ref, acc_ref,
-                    hbuf, wbuf, acc, stage, mrun, srun, stst, qeven, qodd, mrow, irow, mcol, icol,
-                    hsem, wsem, qsem, qbsem, ssd, sss, lsd, lss, rsd, rss):
+                    hbuf, wbuf, acc, stage, mrun, srun, stst, qeven, qodd, x_smem, mrow, irow, mcol, icol,
+                    xsem, hsem, wsem, qsem, qbsem, ssd, sss, lsd, lss, rsd, rss):
     npos = draft + 1
     chips = n_dev // CORES
     seq_dev = h_ref.shape[1] // n_dev
@@ -134,7 +134,7 @@
         m8, i8 = lane_column(mrow[...], b), lane_column(irow[...], b)
         rows = pl.multiple_of(b * 8, 8)
         first = me * seq_dev + b
-        ratio = accept_ratio(draft, [x_ref[i, first] for i in range(draft)],
+        ratio = accept_ratio(draft, [x_smem[i, first] for i in range(draft)],
                              lambda pair, row: za_ref[pair, pl.ds(rows + row, 1), :],
                              lambda pair, row: q_buf[pair, pl.ds(row, 1), :], m8, i8)
         lane = lax.broadcasted_iota(jnp.int32, acc_ref.shape, 1)
@@ -178,6 +178,8 @@
     for k in range(depth_steps):
         start_all(h_copies(0, 0, k, far))
         w_copy(0, k).start()
+    x_copy = pltpu.make_async_copy(x_ref, x_smem, xsem)
+    x_copy.start()
 
     barrier = pltpu.get_barrier_semaphore()
     for o in range(1, n_dev):
@@ -327,6 +329,7 @@
                         for unit in range(UNITS):
                             wait_sent(stat_pieces(0, unit))
                         wait_received(0)
+                        x_copy.wait()
                         for ref, value in zip((mrow, irow, mcol, icol), row_stats(draft, [st_ref[0, n] for n in range(n_dev)], seq_part)):
                             ref[...] = value
                         acc_ref[...] = jnp.zeros(acc_ref.shape, jnp.float32)
@@ -347,8 +350,8 @@
     wait_received(1)
 
 
-def finish_kernel(draft, x_ref, st_ref, acca_ref, ra_ref, zb_ref, q_ref, acc_ref, exp_ref, res_ref, bon_ref,
-                  rb, bonb, mrow, irow, mcol, icol, rsem, bsem):
+def finish_kernel(draft, x_ref, st_ref, acca_ref, ra_ref, zb_ref, q_ref, acc_out, exp_out, res_ref, bon_ref,
+                  rb, bonb, acc_ref, exp_ref, x_smem, mrow, irow, mcol, icol, rsem, bsem, xsem, asem):
     blocks = zb_ref.shape[0]
     seq_part, _, rows_tile, _ = q_ref.shape
     lane_blocks = rows_tile // draft
@@ -375,6 +378,8 @@
         at = pl.ds(g * width, width)
         return pltpu.make_async_copy(bonb.at[:, at], bon_ref.at[strips:, at], bsem.at[strips + g])
 
+    x_copy = pltpu.make_async_copy(x_ref, x_smem, xsem)
+    x_copy.start()
     for b in range(seq_part):
         out_copy_a(b).start()
     for n in range(strips):
@@ -384,6 +389,7 @@
         ref[...] = value
     lane_b = lax.broadcasted_iota(jnp.int32, acc_ref.shape, 1)
     acc_ref[...] = acca_ref[:, :acc_ref.shape[1]]
+    x_copy.wait()
 
     @pl.loop(0, seq_part // group)
     def _(g):
@@ -393,7 +399,7 @@
         at_rows = [pl.ds(pl.multiple_of(b * 8, 8), 8) for b in seqs]
         picked = acc_ref[...]
         for n, b in enumerate(seqs):
-            ratio = accept_ratio(draft, [x_ref[i, first + b] for i in range(draft)],
+            ratio = accept_ratio(draft, [x_smem[i, first + b] for i in range(draft)],
                                  lambda pair, row: zb_ref[pair, pl.ds(b * 8 + row, 1), :],
                                  lambda pair, row: q_ref[b, pair, pl.ds(row, 1), :], m8[n], i8[n])
             picked = jnp.where(lane_b == seq_part + b, ratio, picked)
@@ -440,7 +446,12 @@
         run = run * acc_ref[i:i + 1, :]
         total += run
     exp_ref[...] = total
-
+    small = [pltpu.make_async_copy(src, dst, asem.at[n]) for n, (src, dst) in enumerate(((acc_ref, acc_out), (exp_ref, exp_out)))]
+    for copy in small:
+        copy.start()
+
+    for copy in small:
+        copy.wait()
     for n in range(strips):
         bonus_copy_a(n).wait()
     for b in range(seq_part):
@@ -467,7 +478,6 @@
         rows_block = seq_part * (rows_tile + TILE // LANES)
         any_spec = pl.BlockSpec(memory_space=pl.ANY)
         vmem_spec = pl.BlockSpec(memory_space=pltpu.VMEM)
-        smem_spec = pl.BlockSpec(memory_space=pltpu.SMEM)
         tokens = x_group.T
         q4 = q_rows.reshape(seq_dev, draft, blocks, LANES).transpose(0, 2, 1, 3).reshape(seq_dev, vocab // TILE, rows_tile, LANES)
         stat_scratch = [pltpu.VMEM((8, LANES), f32)] * 2 + [pltpu.VMEM((seq_part, LANES), f32)] * 2
@@ -475,7 +485,7 @@
             functools.partial(exchange_kernel, draft, n_dev),
             out_shape=[pltpu.VMEM((vocab // TILE, rows_block, LANES), f32)] * 2 + [pltpu.VMEM((seq_part, vocab // TILE, rows_tile, LANES), f32)]
                       + [pltpu.VMEM((PHASES, n_dev, 8, LANES), f32), pltpu.VMEM((draft, LANES), f32)],
-            in_specs=[any_spec] * 3 + [smem_spec],
+            in_specs=[any_spec] * 4,
             out_specs=[vmem_spec] * 5,
             scratch_shapes=[
                 pltpu.VMEM((UNITS, npos, seq_unit, depth), hidden.dtype),
@@ -487,8 +497,8 @@
                 pltpu.VMEM((PHASES, UNITS, PEERS, 8, LANES), f32),
                 pltpu.VMEM((vocab // TILE, rows_tile, LANES), f32),
                 pltpu.VMEM((vocab // TILE, rows_tile, LANES), f32),
-                *stat_scratch,
-                dma((UNITS, PEERS, ksteps)), dma((2, ksteps)), dma((2,)), dma((seq_part,)),
+                pltpu.SMEM((draft, seqs), jnp.int32), *stat_scratch,
+                dma, dma((UNITS, PEERS, ksteps)), dma((2, ksteps)), dma((2,)), dma((seq_part,)),
                 dma((SLOTS, UNITS, PEERS)), dma((PHASES, UNITS, PEERS)), dma((SLOTS,)), dma((PHASES,)),
                 dma((PHASES, n_dev)), dma((PHASES, n_dev)),
             ],
@@ -503,11 +513,12 @@
             out_shape=[jax.ShapeDtypeStruct((draft, seq_dev), f32), jax.ShapeDtypeStruct((1, seq_dev), f32),
                        jax.ShapeDtypeStruct((seq_dev, vocab // TILE, rows_tile, LANES), f32),
                        jax.ShapeDtypeStruct((seq_dev // 8, vocab // TILE, TILE // LANES * 8, LANES), f32)],
-            in_specs=[smem_spec] + [vmem_spec] * 5,
-            out_specs=[vmem_spec] * 2 + [any_spec] * 2,
+            in_specs=[any_spec] + [vmem_spec] * 5,
+            out_specs=[any_spec] * 4,
             scratch_shapes=[
-                pltpu.VMEM((seq_part, vocab // TILE, rows_tile, LANES), f32), pltpu.VMEM((seq_part // 8, vocab // TILE, TILE // LANES * 8, LANES), f32), *stat_scratch,
-                dma((seq_dev,)), dma((seq_part // 8 + seq_part // 4,)),
+                pltpu.VMEM((seq_part, vocab // TILE, rows_tile, LANES), f32), pltpu.VMEM((seq_part // 8, vocab // TILE, TILE // LANES * 8, LANES), f32),
+                pltpu.VMEM((draft, seq_dev), f32), pltpu.VMEM((1, seq_dev), f32), pltpu.SMEM((draft, seqs), jnp.int32), *stat_scratch,
+                dma((seq_dev,)), dma((seq_part // 8 + seq_part // 4,)), dma, dma((2,)),
             ],
             compiler_params=pltpu.CompilerParams(vmem_limit_bytes=VMEM_LIMIT),
             cost_estimate=pl.CostEstimate(flops=seq_dev * npos * vocab * 8, bytes_accessed=14 * seq_dev * vocab * 4, transcendentals=seq_dev * npos * vocab),

time: 247 us -> 246 us (level)
  no operation moved by 1% of the time
where the time goes in v5:
time: 246 us; the launch traced here: 245 us
  Pallas kernels  245 us (100%)
    pallas_call x1, Pallas kernels, local_step(): pl.pallas_call(functools.partial(exchange_kernel, draft, n_dev), out_shap...  237 us
    pallas_call x1, Pallas kernels, local_step(): pl.pallas_call(functools.partial(finish_kernel, draft), out_shape=[jax.Sh...  7.7 us

profile of v5, /device:TPU:113, one launch (start us, length us, event | category | flops | bytes accessed | tf_op | source)
XLA Modules:
  0.0 245.4 jit_solution(17201145825617662129)
XLA Ops:
  0.6 237.1 %head_exchange.1 = (f32[128,160,128]{2,1,0:T(8,128)S(1)}, f32[128,160,128]{2,1,0:T(8,128)S(1)}, f32[16,128,8,128]{3,2,1,0:T(8,128)S(1)}, f32[2,8,8,128]{3,2,1,0:T(8,128)S(1)}, f32[4,128]{1,0:T(4,128)S(1)}) custom-call(bf16[5,256,12288]{2,1,0:T(8,128)(2,1)} %bitcast.21, bf16[12288,4096]{1,0:T(8,128)(2,1)} %w_ref.1, f32[32,128,8,128]{3,2,1,0:T(8,128)} %bitcast.22, ...), custom_call_target="tpu_custom_call" | custom-call | flops 128849018880 | bytes 100663296 | tf_op jit(solution)/shard_map/head_exchange/pallas_call | solution.py:484
  237.7 7.7 %finish_rows.1 = (f32[4,32]{1,0:T(4,128)}, f32[1,32]{1,0:T(1,128)}, f32[32,128,8,128]{3,2,1,0:T(8,128)}, f32[4,128,16,128]{3,2,1,0:T(8,128)}) custom-call(s32[4,256]{1,0:T(4,128)} %bitcast.20, f32[2,8,8,128]{3,2,1,0:T(8,128)S(1)} %get-tuple-element.13.st_ref, f32[4,128]{1,0:T(4,128)S(1)} %get-tuple-element.14.acca_ref, ...), custom_call_target="tpu_custom_call" | custom-call | flops 41943040 | bytes 58720256 | tf_op jit(solution)/shard_map/finish_rows/pallas_call | solution.py:511
